TPU v7x, 32 devices: a whole 2x2x4 slice. The times are simulated.
32 devices in a mesh: dp: 8 (over z, x), tp: 4 (over y, core).
Axes of the slice: x: 2, y: 2, z: 4, core: 2. Of those that a mesh axis runs over, the one named last changes fastest.
Arguments:
- main: bfloat16 [16512, 1152], P('dp', 'tp'), may hold values from -6 to 6
- long_skip: bfloat16 [16512, 1152], P('dp', 'tp'), may hold values from -6 to 6
- cotangent: bfloat16 [16512, 1152], P('dp', 'tp'), may hold values from -6 to 6
- timesteps: int32 [64], P('dp'), may hold values from 0 to 999
- loss_codes: int32 [64], P('dp'), may hold values from 0 to 7
- code_weights: float32 [8], replicated, may hold values from 0.25 to 4
- item_counts: int32 [8], P('dp'), may hold values from 4 to 8, as said below
- w_skip_main: bfloat16 [1152, 1152], P('tp'), may hold values from -0.125 to 0.125
- w_skip_long: bfloat16 [1152, 1152], P('tp'), may hold values from -0.125 to 0.125
- b_skip: float32 [1152], P('tp'), may hold values from -3 to 3
- ln1_gain: float32 [1152], P('tp'), may hold values from 0.25 to 1.75
- ln1_bias: float32 [1152], P('tp'), may hold values from -2.4 to 2.4
- w_qkv: bfloat16 [3, 1152, 1152], P(None, None, 'tp'), may hold values from -0.1875 to 0.1875
- w_proj: bfloat16 [1152, 1152], P('tp'), may hold values from -1.5 to 1.5
- b_proj: float32 [1152], P('tp'), may hold values from -3 to 3
- ln2_gain: float32 [1152], P('tp'), may hold values from 0.25 to 1.75
- ln2_bias: float32 [1152], P('tp'), may hold values from -2.4 to 2.4
- w_up: bfloat16 [1152, 4608], P(None, 'tp'), may hold values from -0.1875 to 0.1875
- b_up: float32 [4608], P('tp'), may hold values from -3 to 3
- w_down: bfloat16 [4608, 1152], P('tp'), may hold values from -0.09375 to 0.09375
- b_down: float32 [1152], P('tp'), may hold values from -3 to 3
Outputs:
- out: bfloat16 [16512, 1152], P('dp', 'tp')
- d_main: bfloat16 [16512, 1152], P('dp', 'tp')
- d_long: bfloat16 [16512, 1152], P('dp', 'tp')
- g_w_skip_main: float32 [1152, 1152], P('tp')
- g_w_skip_long: float32 [1152, 1152], P('tp')
- g_b_skip: float32 [1152], P('tp')
- g_ln1_gain: float32 [1152], P('tp')
- g_ln1_bias: float32 [1152], P('tp')
- g_w_qkv: float32 [3, 1152, 1152], P(None, None, 'tp')
- g_w_proj: float32 [1152, 1152], P('tp')
- g_b_proj: float32 [1152], P('tp')
- g_ln2_gain: float32 [1152], P('tp')
- g_ln2_bias: float32 [1152], P('tp')
- g_w_up: float32 [1152, 4608], P(None, 'tp')
- g_b_up: float32 [4608], P('tp')
- g_w_down: float32 [4608, 1152], P('tp')
- g_b_down: float32 [1152], P('tp')
Inputs may be any that keep to these rules, and one draw needn't show every extreme that they name: `item_counts`: each batch group holds 4 to 8 items; some group is full and some holds exactly 4.
All inputs are finite; a program needn't handle non-finite values.
Results may differ from a plain program's by a relative error of at most 0.02.
Values may be sent and summed in bfloat16 or wider, within the bound.
A program may use at most 192 MiB of HBM per device.

v0:
```python
import functools
import math

import jax
import jax.numpy as jnp
from jax import lax
from jax.experimental import pallas as pl
from jax.experimental.pallas import tpu as pltpu
from jax.sharding import PartitionSpec as P

HEAD = 72
SEQ = 258
TSTEPS = 1000


EPSILON = 1e-06
ROOT_HALF = 0.7071067811865476
DENSITY_SCALE = 0.3989422804014327


def item_factors(timesteps, loss_codes, code_weights, group_items):
    steps_float = timesteps.astype(jnp.float32)
    phase = (steps_float / TSTEPS + 0.008) / 1.008 * (math.pi / 2.0)
    cosine = jnp.cos(phase)
    signal = cosine * cosine
    weight = jnp.minimum(1.0, 5.0 * (1.0 - signal) / signal)
    picks = (
        loss_codes[:, None] == jnp.arange(code_weights.shape[0], dtype=jnp.int32)[None, :]
    ).astype(jnp.float32)
    coded = jnp.sum(picks * code_weights[None, :], axis=1)
    valid = (jnp.arange(timesteps.shape[0], dtype=jnp.int32) < group_items).astype(jnp.float32)
    return (weight * coded * valid, valid)


def layer_norm(stream, gain, bias, width):
    totals, squares = lax.psum((jnp.sum(stream, 0), jnp.sum(stream * stream, 0)), "tp")
    mean = totals / width
    rstd = lax.rsqrt(squares / width - mean * mean + EPSILON)
    normed = (stream - mean[None, :]) * rstd[None, :]
    rounded = (normed * gain[:, None] + bias[:, None]).astype(jnp.bfloat16)
    return (normed, rstd, lax.all_gather(rounded, "tp", axis=0, tiled=True))


def norm_back(d_normed, normed, rstd, gain, width):
    g_gain = jnp.sum(d_normed * normed, 1)
    g_bias = jnp.sum(d_normed, 1)
    scaled = d_normed * gain[:, None]
    first, second = lax.psum((jnp.sum(scaled, 0), jnp.sum(scaled * normed, 0)), "tp")
    back = rstd[None, :] * (scaled - first[None, :] / width - normed * second[None, :] / width)
    return (back, g_gain, g_bias)


def reduce_back(term, local_width):
    return lax.psum_scatter(
        term(jnp.int32(0), lax.axis_size("tp") * local_width).astype(jnp.bfloat16),
        "tp",
        scatter_dimension=0,
        tiled=True,
    ).astype(jnp.float32)


def fold_back(shard, pairs):
    piece = lax.all_gather(shard, "tp", axis=0, tiled=True)
    new_acts = tuple(
        (
            jnp.einsum("fc,ct->ft", weight, piece, preferred_element_type=jnp.float32)
            for weight, acts in pairs
        )
    )
    new_weights = tuple(
        (
            jnp.einsum("ft,ct->fc", acts, piece, preferred_element_type=jnp.float32)
            for weight, acts in pairs
        )
    )
    return (new_acts, new_weights)


def split_heads(flat, heads_here):
    pair_count = flat.shape[1] // (2 * SEQ)
    shaped = flat.reshape(heads_here, HEAD, pair_count, 2, SEQ)
    return jnp.moveaxis(shaped, 2, 0)


def join_heads(blocks):
    moved = jnp.moveaxis(blocks, 0, 2)
    return moved.reshape(moved.shape[0] * moved.shape[1], -1)


def attend(block):
    query_rows, key_rows, value_rows = block
    scale = 1.0 / math.sqrt(HEAD)
    scores = (
        jnp.einsum("hdbi,hdbj->hbij", query_rows, key_rows, preferred_element_type=jnp.float32)
        * scale
    )
    peak = jnp.max(scores, axis=-1, keepdims=True)
    logsum = peak + jnp.log(jnp.sum(jnp.exp(scores - peak), axis=-1, keepdims=True))
    probs = jnp.exp(scores - logsum).astype(jnp.bfloat16)
    attended = jnp.einsum("hbij,hdbj->hdbi", probs, value_rows, preferred_element_type=jnp.float32)
    return (attended.astype(jnp.bfloat16), logsum[..., 0])


def attend_back(block):
    query_rows, key_rows, value_rows, logsum, d_attended = block
    scale = 1.0 / math.sqrt(HEAD)
    scores = (
        jnp.einsum("hdbi,hdbj->hbij", query_rows, key_rows, preferred_element_type=jnp.float32)
        * scale
    )
    probs = jnp.exp(scores - logsum[..., None])
    probs_low = probs.astype(jnp.bfloat16)
    d_probs = jnp.einsum(
        "hdbi,hdbj->hbij", d_attended, value_rows, preferred_element_type=jnp.float32
    )
    delta = jnp.sum(probs * d_probs, axis=-1, keepdims=True)
    d_scores = (probs * (d_probs - delta)).astype(jnp.bfloat16)
    d_query = (
        jnp.einsum("hbij,hdbj->hdbi", d_scores, key_rows, preferred_element_type=jnp.float32)
        * scale
    )
    d_key = (
        jnp.einsum("hbij,hdbi->hdbj", d_scores, query_rows, preferred_element_type=jnp.float32)
        * scale
    )
    d_value = jnp.einsum(
        "hbij,hdbi->hdbj", probs_low, d_attended, preferred_element_type=jnp.float32
    )
    return (d_query.astype(jnp.bfloat16), d_key.astype(jnp.bfloat16), d_value.astype(jnp.bfloat16))


def body_features(
    main,
    long_skip,
    cotangent,
    timesteps,
    loss_codes,
    code_weights,
    item_counts,
    w_skip_main,
    w_skip_long,
    b_skip,
    ln1_gain,
    ln1_bias,
    w_qkv,
    w_proj,
    b_proj,
    ln2_gain,
    ln2_bias,
    w_up,
    b_up,
    w_down,
    b_down,
):
    local_width = main.shape[1]
    width = w_skip_main.shape[1]
    heads_here = local_width // HEAD
    item_scale, valid = item_factors(timesteps, loss_codes, code_weights, item_counts[0])
    row_scale = jnp.repeat(item_scale, SEQ)
    row_valid = jnp.repeat(valid, SEQ)
    main_cols = main.T
    long_cols = long_skip.T
    stream = (
        lax.psum_scatter(
            jnp.einsum("dc,dt->ct", w_skip_main, main_cols, preferred_element_type=jnp.float32)
            + jnp.einsum("dc,dt->ct", w_skip_long, long_cols, preferred_element_type=jnp.float32),
            "tp",
            scatter_dimension=0,
            tiled=True,
        )
        + b_skip[:, None]
    )
    normed_one, rstd_one, full_one = layer_norm(stream, ln1_gain, ln1_bias, width)
    qkv = jnp.einsum("edc,dt->ect", w_qkv, full_one, preferred_element_type=jnp.float32).astype(
        jnp.bfloat16
    )
    query_blocks = split_heads(qkv[0], heads_here)
    key_blocks = split_heads(qkv[1], heads_here)
    value_blocks = split_heads(qkv[2], heads_here)
    attended_blocks, logsums = lax.map(attend, (query_blocks, key_blocks, value_blocks))
    attended = join_heads(attended_blocks)
    cols_here = w_proj
    projected = lax.psum_scatter(
        jnp.einsum("rc,rt->ct", cols_here, attended, preferred_element_type=jnp.float32).astype(
            jnp.bfloat16
        ),
        "tp",
        scatter_dimension=0,
        tiled=True,
    ).astype(jnp.float32)
    stream_two = stream + projected + b_proj[:, None]
    normed_two, rstd_two, full_two = layer_norm(stream_two, ln2_gain, ln2_bias, width)
    upward = (
        jnp.einsum("dc,dt->ct", w_up, full_two, preferred_element_type=jnp.float32) + b_up[:, None]
    )
    activated = jax.nn.gelu(upward, approximate=False).astype(jnp.bfloat16)
    cols_here = w_down
    result = (
        stream_two
        + lax.psum_scatter(
            jnp.einsum(
                "fc,ft->ct", cols_here, activated, preferred_element_type=jnp.float32
            ).astype(jnp.bfloat16),
            "tp",
            scatter_dimension=0,
            tiled=True,
        ).astype(jnp.float32)
        + b_down[:, None]
    )
    out = (result * row_valid[None, :]).T.astype(jnp.bfloat16)
    grad_low = (cotangent.T.astype(jnp.float32) * row_scale[None, :]).astype(jnp.bfloat16)
    grad_wide = grad_low.astype(jnp.float32)
    g_b_down = jnp.sum(grad_wide, 1)
    (d_activated,), (g_w_down,) = fold_back(grad_low, ((w_down, activated),))
    cumulative = 0.5 * (1.0 + lax.erf(upward * ROOT_HALF))
    density = jnp.exp(-0.5 * upward * upward) * DENSITY_SCALE
    d_upward = (d_activated * (cumulative + upward * density)).astype(jnp.bfloat16)
    g_b_up = jnp.sum(d_upward.astype(jnp.float32), 1)
    g_w_up = jnp.einsum("dt,ft->df", full_two, d_upward, preferred_element_type=jnp.float32)

    def up_term(start, count_rows):
        return jnp.einsum("cf,ft->ct", w_up, d_upward, preferred_element_type=jnp.float32)

    d_normed_two = reduce_back(up_term, local_width)
    back_two, g_ln2_gain, g_ln2_bias = norm_back(
        d_normed_two, normed_two, rstd_two, ln2_gain, width
    )
    d_stream_two = (back_two + grad_wide).astype(jnp.bfloat16)
    d_stream_wide = d_stream_two.astype(jnp.float32)
    g_b_proj = jnp.sum(d_stream_wide, 1)
    (d_attended,), (g_w_proj,) = fold_back(d_stream_two, ((w_proj, attended),))
    d_attended_blocks = split_heads(d_attended.astype(jnp.bfloat16), heads_here)
    d_queries, d_keys, d_values = lax.map(
        attend_back, (query_blocks, key_blocks, value_blocks, logsums, d_attended_blocks)
    )
    d_qkv = jnp.stack([join_heads(d_queries), join_heads(d_keys), join_heads(d_values)], axis=0)
    g_w_qkv = jnp.einsum("dt,ect->edc", full_one, d_qkv, preferred_element_type=jnp.float32)

    def qkv_term(start, count_rows):
        return jnp.einsum("ecr,ert->ct", w_qkv, d_qkv, preferred_element_type=jnp.float32)

    d_normed_one = reduce_back(qkv_term, local_width)
    back_one, g_ln1_gain, g_ln1_bias = norm_back(
        d_normed_one, normed_one, rstd_one, ln1_gain, width
    )
    d_stream = (back_one + d_stream_wide).astype(jnp.bfloat16)
    g_b_skip = jnp.sum(d_stream.astype(jnp.float32), 1)
    (d_main_cols, d_long_cols), (g_w_main, g_w_long) = fold_back(
        d_stream, ((w_skip_main, main_cols), (w_skip_long, long_cols))
    )
    (
        g_w_main,
        g_w_long,
        g_b_skip,
        g_ln1_gain,
        g_ln1_bias,
        g_w_qkv,
        g_w_proj,
        g_b_proj,
        g_ln2_gain,
        g_ln2_bias,
        g_w_up,
        g_b_up,
        g_w_down,
        g_b_down,
    ) = (
        lax.psum(g_w_main.astype(jnp.bfloat16), "dp").astype(jnp.float32),
        lax.psum(g_w_long.astype(jnp.bfloat16), "dp").astype(jnp.float32),
        lax.psum(g_b_skip.astype(jnp.bfloat16), "dp").astype(jnp.float32),
        lax.psum(g_ln1_gain.astype(jnp.bfloat16), "dp").astype(jnp.float32),
        lax.psum(g_ln1_bias.astype(jnp.bfloat16), "dp").astype(jnp.float32),
        lax.psum(g_w_qkv.astype(jnp.bfloat16), "dp").astype(jnp.float32),
        lax.psum(g_w_proj.astype(jnp.bfloat16), "dp").astype(jnp.float32),
        lax.psum(g_b_proj.astype(jnp.bfloat16), "dp").astype(jnp.float32),
        lax.psum(g_ln2_gain.astype(jnp.bfloat16), "dp").astype(jnp.float32),
        lax.psum(g_ln2_bias.astype(jnp.bfloat16), "dp").astype(jnp.float32),
        lax.psum(g_w_up.astype(jnp.bfloat16), "dp").astype(jnp.float32),
        lax.psum(g_b_up.astype(jnp.bfloat16), "dp").astype(jnp.float32),
        lax.psum(g_w_down.astype(jnp.bfloat16), "dp").astype(jnp.float32),
        lax.psum(g_b_down.astype(jnp.bfloat16), "dp").astype(jnp.float32),
    )
    d_main = d_main_cols.T.astype(jnp.bfloat16)
    d_long = d_long_cols.T.astype(jnp.bfloat16)
    return (
        out,
        d_main,
        d_long,
        g_w_main,
        g_w_long,
        g_b_skip,
        g_ln1_gain,
        g_ln1_bias,
        g_w_qkv,
        g_w_proj,
        g_b_proj,
        g_ln2_gain,
        g_ln2_bias,
        g_w_up,
        g_b_up,
        g_w_down,
        g_b_down,
    )


ITEM_ROWS = 264
GRAD_ROWS = 24
CORE = ("tp", 1)
ACROSS_Y = ("tp", 2)
ACROSS_X = ("dp", 1)
ACROSS_Z = ("dp", 2)


def swap(value, link):
    axis, bit = link
    return lax.ppermute(value, axis, [(i, i ^ bit) for i in range(lax.axis_size(axis))])


def side(link):
    axis, bit = link
    return (lax.axis_index(axis) // bit) % 2


def in_order(bit, mine, theirs):
    flip = bit == 1
    return jnp.stack([jnp.where(flip, theirs, mine), jnp.where(flip, mine, theirs)])


def pick(value, index):
    return lax.dynamic_index_in_dim(value, index, 0, keepdims=False)


def peer(value, bit):
    return value + bit - 2 * bit * ((value // bit) % 2)


def greet(peers):
    barrier = pltpu.get_barrier_semaphore()
    for where in peers:
        pl.semaphore_signal(barrier, inc=1, device_id=where, device_id_type=pl.DeviceIdType.MESH)
    pl.semaphore_wait(barrier, len(peers))


def send(source, target, sems, index, where):
    return pltpu.make_async_remote_copy(
        src_ref=source,
        dst_ref=target,
        send_sem=sems.at[0, index],
        recv_sem=sems.at[1, index],
        device_id=where,
        device_id_type=pl.DeviceIdType.MESH,
    )


def gather_kernel(pieces, n_in, n_out, *refs):
    tokens, vectors, inputs = refs[0], refs[1], refs[2 : 2 + n_in]
    refs = refs[2 + n_in :]
    far_tokens, core_near, core_far, far_vectors, core_vectors = refs[:5]
    outs, held = refs[5 : 5 + n_out], refs[5 + n_out : 5 + n_out + n_in]
    y_sem, one_sem, two_sem, own_sem, far_sem, local_sem, token_sem = refs[5 + n_out + n_in :]
    n = len(pieces)
    shards = [inputs[a].at[lead] if lead else inputs[a] for a, lead, _, _ in pieces]
    stage = [held[a].at[lead] if lead else held[a] for a, lead, _, _ in pieces]
    fulls = [
        [outs[b[place]].at[tail] if isinstance(b, tuple) else outs[b].at[(place,) + tail] for place in range(4)]
        for _, _, b, tail in pieces
    ]
    dp, tp = lax.axis_index("dp"), lax.axis_index("tp")
    core, y = tp % 2, (tp // 2) % 2
    to_core, to_y = {"tp": peer(tp, 1)}, {"tp": peer(tp, 2)}
    links = ({"dp": peer(dp, 1)}, {"dp": peer(dp, 2)})
    bits = (dp % 2, (dp // 2) % 2)
    greet((to_core, to_y) + links)

    def places(k):
        return k % 2, 1 - k % 2, bits[k % 2], bits[1 - k % 2]

    def y_copy(k):
        _, _, f, s = places(k)
        return send(shards[k].at[s, f], fulls[k][1].at[s, f], y_sem, k, to_y)

    def one_copy(k):
        first, _, f, s = places(k)
        part = fulls[k][1].at[s, f]
        return send(part, part, one_sem, k, links[first])

    def two_copy(k):
        _, second, _, s = places(k)
        part = fulls[k][1].at[s]
        return send(part, part, two_sem, k, links[second])

    def own_copy(k):
        return send(shards[k], fulls[k][2], own_sem, k, to_core)

    def far_copy(k):
        return send(fulls[k][1], fulls[k][3], far_sem, k, to_core)

    def load(k):
        return pltpu.make_async_copy(shards[k], stage[k], local_sem.at[0, k])

    def store(k):
        return pltpu.make_async_copy(stage[k], fulls[k][0], local_sem.at[1, k])

    token_y = send(tokens.at[1 - y], far_tokens, token_sem, 0, to_y)
    token_near = send(tokens.at[y, 1 - core], core_near, token_sem, 1, to_core)
    token_far = send(far_tokens.at[1 - core], core_far, token_sem, 2, to_core)
    vectors_y = send(vectors, far_vectors, token_sem, 3, to_y)
    vectors_near = send(vectors, core_vectors.at[0], token_sem, 4, to_core)
    vectors_far = send(far_vectors, core_vectors.at[1], token_sem, 5, to_core)
    vectors_y.start()
    vectors_near.start()
    for k in range(n):
        y_copy(k).start()
    token_y.start()
    token_near.start()
    for k in range(n):
        load(k).start()
        own_copy(k).start()
    for step in range(n + 2):
        if step < n:
            y_copy(step).wait_recv()
            one_copy(step).start()
            load(step).wait()
            store(step).start()
        if 0 <= step - 1 < n:
            one_copy(step - 1).wait_recv()
            two_copy(step - 1).start()
        if 0 <= step - 2 < n:
            two_copy(step - 2).wait_recv()
            far_copy(step - 2).start()
    vectors_y.wait_recv()
    vectors_far.start()
    token_y.wait_recv()
    token_far.start()
    for copy in (token_near, token_far, vectors_near, vectors_far):
        copy.wait()
    token_y.wait_send()
    vectors_y.wait_send()
    for k in range(n):
        far_copy(k).wait()
        own_copy(k).wait()
        store(k).wait()
        for copy in (y_copy(k), one_copy(k), two_copy(k)):
            copy.wait_send()


def gather_weights(tokens, vectors, arrays, pieces, out_shapes):
    n = len(pieces)
    shape = lambda dims, like: jax.ShapeDtypeStruct(dims, like.dtype)
    rows = tokens.shape[2:]
    outs = [shape((2,) + rows, tokens), shape(rows, tokens), shape(rows, tokens)]
    outs += [shape(vectors.shape, vectors), shape((2,) + vectors.shape, vectors)]
    outs += [shape(dims, arrays[0]) for dims in out_shapes]
    sems = [pltpu.SemaphoreType.DMA((2, n))] * 6 + [pltpu.SemaphoreType.DMA((2, 6))]
    return pl.pallas_call(
        functools.partial(gather_kernel, pieces, len(arrays), len(out_shapes)),
        out_shape=outs,
        in_specs=[pl.BlockSpec(memory_space=pltpu.MemorySpace.HBM)] * (2 + len(arrays)),
        out_specs=[pl.BlockSpec(memory_space=pltpu.MemorySpace.HBM)] * len(outs),
        scratch_shapes=[pltpu.VMEM(a.shape, a.dtype) for a in arrays] + sems,
        compiler_params=pltpu.CompilerParams(
            collective_id=1, has_side_effects=True, vmem_limit_bytes=32 * 2**20
        ),
        name="gather_weights",
    )(tokens, vectors, *arrays)


def reduce_kernel(sizes, views, n_arrays, *refs):
    ready, arrays, blocks, quarter = refs[0], refs[1 : 1 + n_arrays], refs[1 + n_arrays], refs[2 + n_arrays]
    refs = refs[3 + n_arrays :]
    outs, refs = refs[: 1 + len(views)], refs[1 + len(views) :]
    from_core, y_blocks, own_quarter, z_quarter, x_quarters = refs[:5]
    total, from_y, from_one, half, from_two, from_far, final, part, far_part = refs[5:14]
    y_sem, one_sem, two_sem, far_sem, back_two, back_one, block_sem, load_sem, out_sem = refs[14:]
    chunks, n_ready = total.shape[0], sizes[0]
    dp, tp = lax.axis_index("dp"), lax.axis_index("tp")
    to_core, to_y, to_far = {"tp": peer(tp, 1)}, {"tp": peer(tp, 2)}, {"dp": peer(dp, 4)}
    to_x, to_z = {"dp": peer(dp, 1)}, {"dp": peer(dp, 2)}
    greet((to_core, to_y, to_x, to_z, to_far))

    def plan(s):
        z_first = (s % 4) // 3
        first, second = 1 + z_first, 2 - z_first
        places = (dp // first) % 2, (dp // second) % 2
        return ({"dp": peer(dp, first)}, {"dp": peer(dp, second)}) + places

    def y_copy(s, source):
        return send(source, from_y.at[s - n_ready], y_sem, s - n_ready, to_y)

    def one_copy(s):
        to_one, _, f, _ = plan(s)
        return send(total.at[s, 1 - f], from_one.at[s], one_sem, s, to_one)

    def two_copy(s):
        _, to_two, _, g = plan(s)
        return send(half.at[s, 1 - g], from_two.at[s], two_sem, s, to_two)

    def far_copy(s):
        _, _, _, g = plan(s)
        return send(half.at[s, g], from_far.at[s], far_sem, s, to_far)

    def back_two_copy(s):
        _, to_two, f, g = plan(s)
        part = final.at[s, f, g]
        return send(part, part, back_two, s, to_two)

    def back_one_copy(s):
        to_one, _, f, _ = plan(s)
        part = final.at[s, f]
        return send(part, part, back_one, s, to_one)

    def out_copies(s, act):
        at = 0
        for k, size in enumerate(sizes):

            @pl.when((s >= at) & (s < at + size))
            def _(k=k, at=at):
                act(pltpu.make_async_copy(final.at[s], outs[k].at[s - at], out_sem.at[s]))

            at += size

    quarter_load = pltpu.make_async_copy(quarter, part, load_sem.at[0])
    ready_load = pltpu.make_async_copy(ready, total.at[pl.ds(0, n_ready)], load_sem.at[1])
    ready_load.start()
    quarter_load.start()
    core_blocks = [send(blocks.at[2 + k], from_core.at[k], block_sem, k, to_core) for k in range(2)]
    own_block = send(blocks.at[1], y_blocks.at[0], block_sem, 2, to_y)
    core_block = send(from_core.at[1], y_blocks.at[1], block_sem, 3, to_y)
    quarter_far = send(quarter, far_part, block_sem, 4, to_far)
    quarter_z = send(own_quarter, z_quarter, block_sem, 5, to_z)
    quarter_x = send(own_quarter, x_quarters.at[0], block_sem, 6, to_x)
    quarter_zx = send(z_quarter, x_quarters.at[1], block_sem, 7, to_x)
    quarter_out = pltpu.make_async_copy(part, own_quarter, out_sem.at[chunks])
    loads, at = [], n_ready
    for k, (size, (a, mine, theirs)) in enumerate(zip(sizes[1:], views)):
        source = arrays[a].at[mine]
        loads.append(pltpu.make_async_copy(source, total.at[pl.ds(at, size)], load_sem.at[2 + k]))
        loads[-1].start()
        for r in range(size):
            y_copy(at + r, arrays[a].at[theirs + (r,)]).start()
        at += size
    for copy in core_blocks:
        copy.start()
    own_block.start()
    quarter_far.start()
    for copy in [ready_load, quarter_load] + loads:
        copy.wait()

    def plus(left, right):
        return (left.astype(jnp.float32) + right.astype(jnp.float32)).astype(jnp.bfloat16)

    def step(t, carry):
        @pl.when((t >= n_ready) & (t < chunks))
        def _():
            y_copy(t, total.at[t]).wait_recv()
            total[t] = plus(total[t], from_y[t - n_ready])

        @pl.when(t < chunks)
        def _():
            one_copy(t).start()

        @pl.when((t >= 2) & (t < chunks + 2))
        def _():
            s = t - 2
            _, _, f, _ = plan(s)
            one_copy(s).wait_recv()
            half[s] = plus(total[s, f], from_one[s])
            two_copy(s).start()

        @pl.when((t >= 3) & (t < chunks + 3))
        def _():
            s = t - 3
            _, _, _, g = plan(s)
            two_copy(s).wait_recv()
            half[s, g] = plus(half[s, g], from_two[s])
            far_copy(s).start()

        @pl.when((t >= 5) & (t < chunks + 5))
        def _():
            s = t - 5
            _, _, f, g = plan(s)
            far_copy(s).wait_recv()
            final[s, f, g] = plus(half[s, g], from_far[s])
            back_two_copy(s).start()

        @pl.when((t >= 6) & (t < chunks + 6))
        def _():
            back_two_copy(t - 6).wait_recv()
            back_one_copy(t - 6).start()

        @pl.when((t >= 7) & (t < chunks + 7))
        def _():
            back_one_copy(t - 7).wait_recv()
            out_copies(t - 7, lambda copy: copy.start())

        @pl.when(t == 2)
        def _():
            for copy in core_blocks:
                copy.wait_recv()
            core_block.start()

        @pl.when(t == 8)
        def _():
            quarter_far.wait()
            part[...] = plus(part[...], far_part[...])
            quarter_out.start()

        @pl.when(t == 9)
        def _():
            quarter_out.wait()
            quarter_z.start()
            quarter_x.start()

        @pl.when(t == 18)
        def _():
            quarter_z.wait_recv()
            quarter_zx.start()

        return carry

    lax.fori_loop(0, chunks + 7, step, 0)

    def finish_y(s, carry):
        y_copy(s, total.at[s]).wait_send()
        return carry

    lax.fori_loop(n_ready, chunks, finish_y, 0)

    def finish(s, carry):
        for copy in (one_copy(s), two_copy(s), far_copy(s), back_two_copy(s), back_one_copy(s)):
            copy.wait_send()
        out_copies(s, lambda copy: copy.wait())
        return carry

    lax.fori_loop(0, chunks, finish, 0)
    for copy in core_blocks:
        copy.wait_send()
    own_block.wait()
    core_block.wait()
    quarter_z.wait_send()
    quarter_x.wait()
    quarter_zx.wait()


def reduce_grads(ready, arrays, views, blocks, quarter):
    sizes = (ready.shape[0],) + tuple(arrays[a].shape[len(mine)] for a, mine, _ in views)
    chunks = sum(sizes)
    rows, width = ready.shape[-2:]
    kind = ready.dtype
    sem = lambda n: pltpu.SemaphoreType.DMA((2, n))
    two_blocks = jax.ShapeDtypeStruct((2,) + blocks.shape[1:], blocks.dtype)
    hbm = pl.BlockSpec(memory_space=pltpu.MemorySpace.HBM)
    vmem = lambda *lead: pltpu.VMEM(lead + (rows, width), kind)
    n_in, n_out = 3 + len(arrays), 6 + len(views)
    return pl.pallas_call(
        functools.partial(reduce_kernel, sizes, views, len(arrays)),
        out_shape=[jax.ShapeDtypeStruct((n, 2, 2, rows, width), kind) for n in sizes]
        + [two_blocks, two_blocks]
        + [jax.ShapeDtypeStruct(lead + quarter.shape, kind) for lead in ((), (), (2,))],
        in_specs=[hbm] * n_in,
        out_specs=[hbm] * n_out,
        scratch_shapes=[
            vmem(chunks, 2, 2),
            vmem(chunks - sizes[0], 2, 2),
            vmem(chunks, 2),
            vmem(chunks, 2),
            vmem(chunks),
            vmem(chunks),
            vmem(chunks, 2, 2),
            pltpu.VMEM(quarter.shape, kind),
            pltpu.VMEM(quarter.shape, kind),
            sem(chunks - sizes[0]),
            sem(chunks),
            sem(chunks),
            sem(chunks),
            sem(chunks),
            sem(chunks),
            sem(8),
            pltpu.SemaphoreType.DMA((2 + len(views),)),
            pltpu.SemaphoreType.DMA((chunks + 1,)),
        ],
        compiler_params=pltpu.CompilerParams(
            collective_id=2, has_side_effects=True, vmem_limit_bytes=56 * 2**20
        ),
        name="reduce_grads",
    )(ready, *arrays, blocks, quarter)


def add_low(mine, theirs):
    return (mine.astype(jnp.float32) + theirs.astype(jnp.float32)).astype(jnp.bfloat16)


def place_of(index):
    rank = lax.axis_index("tp")
    core, y = rank % 2, (rank // 2) % 2
    there_core, there_y = index % 2, index // 2
    apart = lambda a, b: a + b - 2 * a * b
    return apart(y, there_y) + 2 * apart(core, there_core)


def spread_kernel(main_ref, long_ref, cot_ref, tokens_ref, cot_tokens_ref):
    cols = main_ref.shape[1]
    items = tokens_ref.shape[1] // ITEM_ROWS
    for p in range(4):
        for i in range(items):
            source = slice((p * items + i) * SEQ, (p * items + i + 1) * SEQ)
            target = slice(i * ITEM_ROWS, i * ITEM_ROWS + SEQ)
            blank = slice(i * ITEM_ROWS + SEQ, (i + 1) * ITEM_ROWS)
            tokens_ref[p, target, :cols] = main_ref[source, :]
            tokens_ref[p, target, cols:] = long_ref[source, :]
            cot_tokens_ref[p, target, :] = cot_ref[source, :]
            tokens_ref[p, blank, :] = jnp.zeros((ITEM_ROWS - SEQ, 2 * cols), tokens_ref.dtype)
            cot_tokens_ref[p, blank, :] = jnp.zeros((ITEM_ROWS - SEQ, cols), tokens_ref.dtype)


def spread(main, long_skip, cotangent):
    rows, cols = main.shape
    padded = rows // SEQ // 4 * ITEM_ROWS
    return pl.pallas_call(
        spread_kernel,
        out_shape=[
            jax.ShapeDtypeStruct((4, padded, 2 * cols), main.dtype),
            jax.ShapeDtypeStruct((4, padded, cols), main.dtype),
        ],
        compiler_params=pltpu.CompilerParams(vmem_limit_bytes=40 * 2**20),
        name="spread",
    )(main, long_skip, cotangent)


def arrange_kernel(own_ref, y_ref, partner_ref, scale_ref, out_ref, held):
    cols = own_ref.shape[1]
    held[0] = own_ref[...]
    held[1] = y_ref[...]
    held[2] = partner_ref[0]
    held[3] = partner_ref[1]
    for j in range(4):
        block = held[place_of(j)].astype(jnp.float32) * scale_ref[...]
        out_ref[:, j * cols : (j + 1) * cols] = block.astype(out_ref.dtype)


def arrange(own, along_y, partner, scale):
    rows, cols = own.shape
    return pl.pallas_call(
        arrange_kernel,
        out_shape=jax.ShapeDtypeStruct((rows, 4 * cols), own.dtype),
        scratch_shapes=[pltpu.VMEM((4, rows, cols), own.dtype)],
        compiler_params=pltpu.CompilerParams(vmem_limit_bytes=24 * 2**20),
        name="arrange",
    )(own, along_y, partner, scale)


def disperse_kernel(rows_ref, valid_ref, out_ref):
    cols = out_ref.shape[2]
    for j in range(4):
        block = rows_ref[:, j * cols : (j + 1) * cols] * valid_ref[...]
        out_ref[place_of(j)] = block.astype(out_ref.dtype)


def disperse(rows, valid):
    count, width = rows.shape
    return pl.pallas_call(
        disperse_kernel,
        out_shape=jax.ShapeDtypeStruct((4, count, width // 4), jnp.bfloat16),
        compiler_params=pltpu.CompilerParams(vmem_limit_bytes=24 * 2**20),
        name="disperse",
    )(rows, valid)


def unspread_kernel(parts, own_ref, core_ref, y_ref, *refs):
    outs, held = refs[:parts], refs[parts]
    cols = outs[0].shape[1]
    items = own_ref.shape[0] // ITEM_ROWS
    held[0] = own_ref[...]
    held[1] = y_ref[0]
    held[2] = core_ref[...]
    held[3] = y_ref[1]
    for p in range(4):
        rows = held[place_of(p)]
        for i in range(items):
            target = slice((p * items + i) * SEQ, (p * items + i + 1) * SEQ)
            source = slice(i * ITEM_ROWS, i * ITEM_ROWS + SEQ)
            for k in range(parts):
                outs[k][target, :] = rows[source, k * cols : (k + 1) * cols]


def unspread(own, core_tokens, y_tokens, parts):
    rows, width = own.shape
    out = jax.ShapeDtypeStruct((4 * rows // ITEM_ROWS * SEQ, width // parts), own.dtype)
    return pl.pallas_call(
        functools.partial(unspread_kernel, parts),
        out_shape=[out] * parts,
        scratch_shapes=[pltpu.VMEM((4, rows, width), own.dtype)],
        compiler_params=pltpu.CompilerParams(vmem_limit_bytes=40 * 2**20),
        name="unspread",
    )(own, core_tokens, y_tokens)


def natural(own_half, partner_half, axis):
    flip_y, flip_core = side(ACROSS_Y) == 1, side(CORE) == 1
    r0, r2 = jnp.split(own_half, 2, axis)
    r1, r3 = jnp.split(partner_half, 2, axis)
    a0, a2 = jnp.where(flip_y, r2, r0), jnp.where(flip_y, r0, r2)
    a1, a3 = jnp.where(flip_y, r3, r1), jnp.where(flip_y, r1, r3)
    b0, b1 = jnp.where(flip_core, a1, a0), jnp.where(flip_core, a0, a1)
    b2, b3 = jnp.where(flip_core, a3, a2), jnp.where(flip_core, a2, a3)
    return (b0, b1, b2, b3)


def dot(spec, left, right):
    return jnp.einsum(spec, left, right, preferred_element_type=jnp.float32)


def low(value):
    return value.astype(jnp.bfloat16)


def norm_rows(stream, gain, bias):
    mean = jnp.mean(stream, 1, keepdims=True)
    square = jnp.mean(stream * stream, 1, keepdims=True)
    rstd = lax.rsqrt(square - mean * mean + EPSILON)
    normed = (stream - mean) * rstd
    return normed, rstd, low(normed * gain + bias)


def norm_rows_back(d_out, normed, rstd, gain):
    g_gain = jnp.sum(d_out * normed, 0)
    g_bias = jnp.sum(d_out, 0)
    scaled = d_out * gain
    first = jnp.mean(scaled, 1, keepdims=True)
    second = jnp.mean(scaled * normed, 1, keepdims=True)
    return rstd * (scaled - first - normed * second), g_gain, g_bias


LAST = (((1,), (1,)), ((), ()))
LEAD = (((0,), (0,)), ((), ()))


def item_scores(key, query):
    scores = lax.dot_general(key, query, LAST, preferred_element_type=jnp.float32)
    present = lax.broadcasted_iota(jnp.int32, scores.shape, 0) < SEQ
    return jnp.where(present, scores * (1.0 / math.sqrt(HEAD)), -1e30)


def attend_kernel(*refs):
    def item(i, carry):
        attend_item(*(ref.at[i] for ref in refs))
        return carry

    lax.fori_loop(0, refs[0].shape[0], item, 0)


def attend_item(q_ref, k_ref, v_ref, out_ref, lse_ref):
    for h in range(q_ref.shape[1] // HEAD):
        at = slice(h * HEAD, (h + 1) * HEAD)
        scores = item_scores(k_ref[:, at], q_ref[:, at])
        peak = jnp.max(scores, axis=0, keepdims=True)
        weights = jnp.exp(scores - peak)
        total = jnp.sum(weights, axis=0, keepdims=True)
        probs = (weights * (1.0 / total)).astype(jnp.bfloat16)
        out = lax.dot_general(probs, v_ref[:, at], LEAD, preferred_element_type=jnp.float32)
        out_ref[:, at] = out.astype(jnp.bfloat16)
        lse_ref[h : h + 1, :] = peak + jnp.log(total)


def attend_back_kernel(*refs):
    def item(i, carry):
        attend_back_item(*(ref.at[i] for ref in refs))
        return carry

    lax.fori_loop(0, refs[0].shape[0], item, 0)


def attend_back_item(q_ref, k_ref, v_ref, lse_ref, d_ref, dq_ref, dk_ref, dv_ref, own_ref, partner_ref):
    scale = 1.0 / math.sqrt(HEAD)
    for h in range(q_ref.shape[1] // HEAD):
        at = slice(h * HEAD, (h + 1) * HEAD)
        query, key, d_out = q_ref[:, at], k_ref[:, at], d_ref[:, at]
        probs = jnp.exp(item_scores(key, query) - lse_ref[h : h + 1, :])
        d_probs = lax.dot_general(v_ref[:, at], d_out, LAST, preferred_element_type=jnp.float32)
        delta = jnp.sum(probs * d_probs, axis=0, keepdims=True)
        d_scores = (probs * (d_probs - delta)).astype(jnp.bfloat16)
        dq = lax.dot_general(d_scores, key, LEAD, preferred_element_type=jnp.float32)
        dk = jnp.dot(d_scores, query, preferred_element_type=jnp.float32)
        dv = jnp.dot(probs.astype(jnp.bfloat16), d_out, preferred_element_type=jnp.float32)
        cols = q_ref.shape[1] // 2
        side_ref, start = (own_ref, h * HEAD) if h * HEAD < cols else (partner_ref, h * HEAD - cols)
        for e, (ref, d) in enumerate(((dq_ref, dq * scale), (dk_ref, dk * scale), (dv_ref, dv))):
            d = d.astype(jnp.bfloat16)
            ref[:, at] = d
            side_ref[:, e * cols + start : e * cols + start + HEAD] = d


def by_item(value):
    return value.reshape(-1, ITEM_ROWS, value.shape[1])


def attention(query, key, value):
    rows, cols = query.shape
    heads, items = cols // HEAD, rows // ITEM_ROWS
    out, lse = pl.pallas_call(
        attend_kernel,
        out_shape=[
            jax.ShapeDtypeStruct((items, ITEM_ROWS, cols), jnp.bfloat16),
            jax.ShapeDtypeStruct((items, heads, ITEM_ROWS), jnp.float32),
        ],
        cost_estimate=pl.CostEstimate(
            flops=4 * rows * ITEM_ROWS * cols, bytes_accessed=8 * rows * cols, transcendentals=rows * ITEM_ROWS * heads
        ),
        compiler_params=pltpu.CompilerParams(vmem_limit_bytes=24 * 2**20),
        name="attend",
    )(by_item(query), by_item(key), by_item(value))
    return out.reshape(rows, cols), lse


def attention_back(query, key, value, lse, d_out):
    rows, cols = query.shape
    heads, items = cols // HEAD, rows // ITEM_ROWS
    shape = lambda width: jax.ShapeDtypeStruct((items, ITEM_ROWS, width), jnp.bfloat16)
    outs = pl.pallas_call(
        attend_back_kernel,
        out_shape=[shape(cols)] * 3 + [shape(3 * cols // 2)] * 2,
        cost_estimate=pl.CostEstimate(
            flops=10 * rows * ITEM_ROWS * cols, bytes_accessed=14 * rows * cols, transcendentals=rows * ITEM_ROWS * heads
        ),
        compiler_params=pltpu.CompilerParams(vmem_limit_bytes=32 * 2**20),
        name="attend_back",
    )(by_item(query), by_item(key), by_item(value), lse, by_item(d_out))
    return [o.reshape(rows, -1) for o in outs]


HIDDEN_BLOCK = 384


def feed_kernel(first, n_ref, g_ref, up_ref, bias_ref, down_ref, *refs):
    sums, (act_ref, d_up_ref, g_bias_ref, result_ref, d_n_ref) = refs[:-5], refs[-5:]
    wide = jnp.float32

    @pl.when(pl.program_id(0) == 0)
    def _():
        result_ref[...] = sums[0][...]
        d_n_ref[...] = jnp.zeros_like(d_n_ref) if first else sums[1][...]

    up = jnp.dot(n_ref[...], up_ref[...], preferred_element_type=wide) + bias_ref[...]
    d_act = lax.dot_general(g_ref[...], down_ref[...], LAST, preferred_element_type=wide)
    cumulative = 0.5 * (1.0 + lax.erf(up * ROOT_HALF))
    density = jnp.exp(-0.5 * up * up) * DENSITY_SCALE
    act = (up * cumulative).astype(jnp.bfloat16)
    d_up = (d_act * (cumulative + up * density)).astype(jnp.bfloat16)
    act_ref[...] = act
    d_up_ref[...] = d_up
    g_bias_ref[...] = jnp.sum(d_up.astype(wide), axis=0, keepdims=True)
    result_ref[...] += jnp.dot(act, down_ref[...], preferred_element_type=wide)
    d_n_ref[...] += lax.dot_general(d_up, up_ref[...], LAST, preferred_element_type=wide)


def feed(n, g, up, bias, down, result, d_n):
    rows, width = n.shape
    hidden = up.shape[1]
    whole = pl.BlockSpec((rows, width), lambda i: (0, 0))
    across = pl.BlockSpec((rows, HIDDEN_BLOCK), lambda i: (0, i))
    line = pl.BlockSpec((1, HIDDEN_BLOCK), lambda i: (0, i))
    sums = (result,) if d_n is None else (result, d_n)
    shape = jax.ShapeDtypeStruct
    return pl.pallas_call(
        functools.partial(feed_kernel, d_n is None),
        grid=(hidden // HIDDEN_BLOCK,),
        out_shape=[
            shape((rows, hidden), jnp.bfloat16),
            shape((rows, hidden), jnp.bfloat16),
            shape((1, hidden), jnp.float32),
            shape((rows, width), jnp.float32),
            shape((rows, width), jnp.float32),
        ],
        in_specs=[
            whole,
            whole,
            pl.BlockSpec((width, HIDDEN_BLOCK), lambda i: (0, i)),
            line,
            pl.BlockSpec((HIDDEN_BLOCK, width), lambda i: (i, 0)),
        ]
        + [whole] * len(sums),
        out_specs=[across, across, line, whole, whole],
        compiler_params=pltpu.CompilerParams(vmem_limit_bytes=40 * 2**20),
        cost_estimate=pl.CostEstimate(
            flops=10 * rows * width * hidden, bytes_accessed=4 * width * hidden, transcendentals=2 * rows * hidden
        ),
        name="feed",
    )(n, g, up, bias, down, *sums)


def body_rows(
    main,
    long_skip,
    cotangent,
    timesteps,
    loss_codes,
    code_weights,
    item_counts,
    w_skip_main,
    w_skip_long,
    b_skip,
    ln1_gain,
    ln1_bias,
    w_qkv,
    w_proj,
    b_proj,
    ln2_gain,
    ln2_bias,
    w_up,
    b_up,
    w_down,
    b_down,
):
    local = main.shape[1]
    width = 4 * local
    rank = lax.axis_index("tp")

    vectors = jnp.concatenate(
        [jnp.stack([b_skip, ln1_gain, ln1_bias, b_proj, ln2_gain, ln2_bias, b_down]), b_up.reshape(4, local)]
    )
    y, core, x, z = side(ACROSS_Y), side(CORE), side(ACROSS_X), side(ACROSS_Z)
    cut = 2 * local
    tokens, cot_tokens = spread(main, long_skip, cotangent)
    tokens = tokens.reshape((2, 2) + tokens.shape[1:])
    cot_tokens = cot_tokens.reshape((2, 2) + cot_tokens.shape[1:])
    quarters = lambda w: w.reshape(2, 2, -1, width)
    qkv_rows = jnp.swapaxes(w_qkv, 1, 2).reshape(3, 2, 2, local // 4, width)
    one = (4, 2, 2, local // 4, width)
    far_tokens, core_near, core_far, far_vectors, core_vectors, wskip, wq, wk, wv, wp, *wu = gather_weights(
        tokens,
        vectors,
        [
            quarters(w_skip_main),
            quarters(w_skip_long),
            qkv_rows,
            quarters(w_proj),
            w_up.reshape(2, 2, 2, width // 8, width),
        ],
        [
            (0, (), 0, (0,)),
            (1, (), 0, (1,)),
            (2, (0,), 1, ()),
            (2, (1,), 2, ()),
            (2, (2,), 3, ()),
            (3, (), 4, ()),
            (4, (0,), (5, 6, 7, 8), (0,)),
            (4, (1,), (5, 6, 7, 8), (1,)),
        ],
        [(4, 2) + one[1:], one, one, one, one] + [(2, 2, 2, width // 8, width)] * 4,
    )
    own_vectors = jnp.concatenate([vectors, far_vectors], axis=1)
    partner_vectors = jnp.concatenate([core_vectors[0], core_vectors[1]], axis=1)
    joined = jnp.concatenate(natural(own_vectors[:7], partner_vectors[:7], 1), axis=1)
    b_skip_all, gain_one, bias_one, b_proj_all, gain_two, bias_two, b_down_all = (
        joined[k : k + 1] for k in range(7)
    )

    def up_vector(pair):
        near, far = jnp.split(pair[7:], 2, 1)
        return jnp.concatenate([near.reshape(1, -1), far.reshape(1, -1)], axis=1)

    b_up_all = jnp.concatenate([up_vector(own_vectors), up_vector(partner_vectors)], axis=1)

    wskip, wq, wk, wv, wp = (g.reshape(-1, width) for g in (wskip, wq, wk, wv, wp))
    wu = [w.reshape(width, width) for w in wu]
    near_tokens = pick(tokens, y)
    skip_rows = jnp.concatenate([pick(near_tokens, core), pick(far_tokens, core), core_near, core_far], axis=1)
    other = lambda value: swap(value, CORE)
    both = lambda mine, others: jnp.concatenate([mine, others], axis=0)
    shares = lambda value: both(value[:, : value.shape[1] // 2], other(value[:, value.shape[1] // 2 :]))

    def after(value, *events):
        return lax.optimization_barrier((value,) + events)[0]

    meet = lambda *values: lax.optimization_barrier(values)

    cot_near = pick(cot_tokens, y)
    cot_far = swap(after(pick(cot_tokens, 1 - y), wskip), ACROSS_Y)
    w_down_then = after(w_down, skip_rows)
    wd_core = other(w_down_then)
    wd_y = swap(w_down_then, ACROSS_Y)

    stream = dot("td,dc->tc", skip_rows, wskip) + b_skip_all
    cot_far, stream = meet(cot_far, stream)
    normed_one, rstd_one, full_one = norm_rows(stream, gain_one, bias_one)
    skip_both = jnp.concatenate([pick(near_tokens, 1 - core), pick(far_tokens, 1 - core)], axis=1)
    skip_both = both(skip_rows[:, : 2 * cut], skip_both)
    n1_both = both(full_one, other(full_one))
    query, key, value = (low(dot("td,cd->tc", full_one, w)) for w in (wq, wk, wv))
    attended, logsum = attention(query, key, value)
    attended_both = shares(attended)
    stream_two = stream + dot("tc,cd->td", attended, wp) + b_proj_all
    stream_two, skip_both, n1_both = meet(stream_two, skip_both, n1_both)
    normed_two, rstd_two, full_two = norm_rows(stream_two, gain_two, bias_two)
    n2_both = both(full_two, other(full_two))
    cot_partner = other(jnp.stack([pick(cot_near, 1 - core), pick(cot_far, 1 - core)]))
    item_scale, valid = item_factors(timesteps, loss_codes, code_weights, item_counts[0])
    row_scale = jnp.repeat(pick(item_scale.reshape(4, -1), rank), ITEM_ROWS)[:, None]
    row_valid = jnp.repeat(pick(valid.reshape(4, -1), rank), ITEM_ROWS)[:, None]
    grad_low = arrange(pick(cot_near, core), pick(cot_far, core), cot_partner, row_scale)
    grad_both = both(grad_low, other(grad_low))
    grad_wide = grad_low.astype(jnp.float32)
    g_b_down = jnp.sum(grad_wide, 0)

    def weight_grad(left, right):
        return low(dot("tf,tc->fc", left, right))

    def split(value, bit):
        halves = value.reshape(2, -1, width)
        return pick(halves, bit), pick(halves, 1 - bit)

    result, d_n2 = stream_two + b_down_all, None
    acts, d_up, g_b_up = [None] * 4, [None] * 4, [None] * 4
    wd_y, stream_two_then = meet(wd_y, result)
    result = stream_two_then
    wd = [w_down, wd_y, wd_core, other(wd_y)]

    def run_feed(r, result, d_n2):
        bias = b_up_all[:, r * width : (r + 1) * width]
        acts[r], d_up[r], g_b_up[r], result, d_n2 = feed(full_two, grad_low, wu[r], bias, wd[r], result, d_n2)
        return result, d_n2

    for r in (1, 3):
        result, d_n2 = run_feed(r, result, d_n2)
    down_theirs = weight_grad(both(acts[1], other(acts[3])), grad_both)
    down_come = swap(down_theirs, ACROSS_Y)
    up_theirs = weight_grad(n2_both, after(both(d_up[1], other(d_up[3])), down_theirs))
    up_come = swap(up_theirs, ACROSS_Y)
    d_n2, up_theirs = meet(d_n2, up_theirs)
    result, d_n2 = run_feed(0, result, d_n2)
    result, d_n2 = run_feed(2, result, d_n2)
    g_b_up = jnp.concatenate(g_b_up)
    down_mine = weight_grad(both(acts[0], other(acts[2])), grad_both)
    up_mine = weight_grad(n2_both, both(d_up[0], other(d_up[2])))
    down_mine, up_mine = meet(down_mine, up_mine)

    outs = disperse(result, row_valid)
    out_core = other(outs[2:])
    out_y = swap(after(jnp.stack([outs[1], out_core[1]]), up_theirs), ACROSS_Y)
    back_two, g_ln2_gain, g_ln2_bias = norm_rows_back(d_n2, normed_two, rstd_two, gain_two)
    d_stream_two = low(back_two + grad_wide)
    d_stream_wide = d_stream_two.astype(jnp.float32)
    g_b_proj = jnp.sum(d_stream_wide, 0)
    chunked = lambda g, lead: g.reshape(lead + (-1, 2, 2, GRAD_ROWS, width))
    proj_part = chunked(weight_grad(attended_both, both(d_stream_two, other(d_stream_two))), (2,))
    d_attended = low(dot("tc,fc->tf", d_stream_two, wp))
    d_qkv = attention_back(query, key, value, logsum, d_attended)
    down_come, *d_qkv = meet(down_come, *d_qkv)
    down_keep, down_send = split(add_low(down_mine, down_come), x)
    down_come = swap(down_send, ACROSS_X)
    *d_qkv, d_own, d_partner = d_qkv
    qkv_part = chunked(weight_grad(both(d_own, other(d_partner)), n1_both), (3, 2))
    d_n1 = sum(dot("tc,cd->td", d, w) for d, w in zip(d_qkv, (wq, wk, wv)))
    back_one, g_ln1_gain, g_ln1_bias = norm_rows_back(d_n1, normed_one, rstd_one, gain_one)
    d_stream = low(back_one + d_stream_wide)
    d_stream_both = both(d_stream, other(d_stream))
    g_b_skip = jnp.sum(d_stream.astype(jnp.float32), 0)
    d_skip = low(dot("tc,fc->tf", d_stream, wskip))
    d_blocks = jnp.stack(jnp.split(d_skip, 4, 1))
    down_come, d_stream_both, d_blocks, proj_part, qkv_part = meet(
        down_come, d_stream_both, d_blocks, proj_part, qkv_part
    )
    down_keep, down_send = split(add_low(down_keep, down_come), z)
    down_come = swap(down_send, ACROSS_Z)
    skip_part = chunked(weight_grad(skip_both, d_stream_both), (2,))
    up_come, down_come, skip_part = meet(up_come, down_come, skip_part)
    down_quarter = add_low(down_keep, down_come)
    ready = chunked(add_low(up_mine, up_come), ())

    small = jnp.stack([g_b_skip, g_ln1_gain, g_ln1_bias, g_b_proj, g_ln2_gain, g_ln2_bias, g_b_down])
    arrived = other(jnp.concatenate([small, g_b_up[2:]]))
    small = jnp.moveaxis((small + arrived[:7]).reshape(7, 4, local), 1, 0)
    b_up_sums = g_b_up[:2] + arrived[7:]

    def vector_rows(shard, row):
        flat = jnp.concatenate([pick(small, shard).reshape(-1), b_up_sums[row]])
        return jnp.pad(flat, (0, 4 * GRAD_ROWS * width - flat.size)).reshape(1, 2, 2, GRAD_ROWS, width)

    vector_part = low(jnp.stack([vector_rows(rank, 0), vector_rows(peer(rank, 2), 1)]))
    g_w_up, *sums = reduce_grads(
        ready,
        [proj_part, qkv_part, vector_part, skip_part],
        [(0, (0,), (1,)), (1, (0, 0), (0, 1)), (1, (1, 0), (1, 1)), (1, (2, 0), (2, 1)), (2, (0,), (1,)), (3, (0,), (1,))],
        d_blocks,
        down_quarter,
    )
    *sums, from_core, y_blocks, down_quarter, z_quarter, x_quarters = sums
    out_y, y_blocks = meet(out_y, y_blocks)
    (out,) = unspread(outs[0], out_core[0], out_y, 1)
    wide = lambda value: value.reshape(-1, width).astype(jnp.float32)
    g_w_down = wide(in_order(x, in_order(z, down_quarter, z_quarter), in_order(z, x_quarters[0], x_quarters[1])))
    g_w_proj, g_q, g_k, g_v, vectors, g_skip = (wide(g) for g in sums)
    g_w_qkv = jnp.stack([g.T for g in (g_q, g_k, g_v)])
    vectors = vectors.reshape(-1)
    mine = vectors[: 7 * local].reshape(7, local)

    d_main, d_long = unspread(d_blocks[0], from_core[0], y_blocks, 2)
    return (
        out,
        d_main,
        d_long,
        g_skip[:local],
        g_skip[local:],
        mine[0],
        mine[1],
        mine[2],
        g_w_qkv,
        g_w_proj,
        mine[3],
        mine[4],
        mine[5],
        wide(g_w_up),
        vectors[7 * local : 7 * local + width],
        g_w_down,
        mine[6],
    )


def body_items(*args):
    return body_rows(*args)


def solution(mesh):
    by_items = mesh.shape["tp"] == 4 and mesh.shape["dp"] == 8
    return jax.shard_map(
        body_items if by_items else body_features,
        mesh=mesh,
        in_specs=(
            P("dp", "tp"),
            P("dp", "tp"),
            P("dp", "tp"),
            P("dp"),
            P("dp"),
            P(),
            P("dp"),
            P("tp", None),
            P("tp", None),
            P("tp"),
            P("tp"),
            P("tp"),
            P(None, None, "tp"),
            P("tp", None),
            P("tp"),
            P("tp"),
            P("tp"),
            P(None, "tp"),
            P("tp"),
            P("tp", None),
            P("tp"),
        ),
        out_specs=(
            P("dp", "tp"),
            P("dp", "tp"),
            P("dp", "tp"),
            P("tp", None),
            P("tp", None),
            P("tp"),
            P("tp"),
            P("tp"),
            P(None, None, "tp"),
            P("tp", None),
            P("tp"),
            P("tp"),
            P("tp"),
            P(None, "tp"),
            P("tp"),
            P("tp", None),
            P("tp"),
        ),
        check_vma=False,
    )
```

profile of v0, /device:TPU:0, one launch (start us, length us, event | category | flops | bytes accessed | tf_op | source)
XLA Modules:
  0.0 644.3 jit_solution(15855328066657547309)
XLA Ops:
  8.8 2.6 copy.74.long_ref
  11.4 2.6 copy.75.cot_ref
  23.7 74.2 %gather_weights.1 = (bf16[2,528,576]{2,1,0:T(8,128)(2,1)S(1)}, bf16[528,576]{1,0:T(8,128)(2,1)S(1)}, bf16[528,576]{1,0:T(8,128)(2,1)S(1)}, f32[11,288]{1,0:T(8,1...) custom-call(bf16[2,2,528,576]{3,2,1,0:T(8,128)(2,1)} %bitcast.149, ...), custom_call_target="tpu_custom_call" | custom-call | tf_op jit(solution)/shard_map/gather_weights/pallas_call | solution.py:454
  109.6 2.7 dynamic-slice_bitcast_fusion.1
  113.6 3.9 concatenate.112
  119.1 6.0 convolution_add_fusion.2
  137.1 9.6 %attend.1 = (bf16[2,264,1152]{2,1,0:T(8,128)(2,1)S(1)}, f32[2,16,264]{2,1,0:T(8,128)S(1)}) custom-call(bf16[2,264,1152]{2,1,0:T(8,128)(2,1)S(1)} %bitcast.178, bf16[2,264,1152]{2,1,0:T(8,128)(2,1)S(1)} %bitcast.176, bf16[2,264,1152]{2,1,0:T(8,128)(2,1)S(1)} %bitcast.174), custom_call_target="tpu_custom_call" | custom-call | flops 642318336 | bytes 4866048 | tf_op jit(solution)/shard_map/attend/pallas_call | solution.py:899
  153.4 31.6 %collective-permute-done.4.down_ref = bf16[1152,1152]{1,0:T(8,128)(2,1)} collective-permute-done((bf16[1152,1152]{1,0:T(8,128)(2,1)}, bf16[1152,1152]{1,0:T(8,128)(2,1)}, u32[]{:S(2)}, u32[]{:S(2)}) %collective-permute-start.4) | collective-permute-done | bytes 2654240 | tf_op jit(solution)/shard_map/ppermute | solution.py:315
  197.2 11.3 %feed.4 = (bf16[528,1152]{1,0:T(8,128)(2,1)S(1)}, bf16[528,1152]{1,0:T(8,128)(2,1)S(1)}, f32[1,1152]{1,0:T(1,128)S(1)}, f32[528,1152]{1,0:T(8,128)S(1)}, f32[528,1152]{1,0:T(8,128)S(1)}) custom-call(bf16[528,1152]{1,0:T(8,128)(2,1)S(1)} %copy-done.22, bf16[528,1152]{1,0:T(8,128)(2,1)S(1)} %arrange.1.g_ref, bf16[1152,1152]{1,0:T(8,128)(2,1)} %bitcast.171, ...), custom_call_target="tpu_custom_call" | custom-call | flops 7007109120 | bytes 5308416 | tf_op jit(solution)/shard_map/feed/pallas_call | solution.py:963
  210.5 11.3 %feed.5 = (bf16[528,1152]{1,0:T(8,128)(2,1)}, bf16[528,1152]{1,0:T(8,128)(2,1)}, f32[1,1152]{1,0:T(1,128)S(1)}, f32[528,1152]{1,0:T(8,128)S(1)}, f32[528,1152]{1,0:T(8,128)S(1)}) custom-call(bf16[528,1152]{1,0:T(8,128)(2,1)S(1)} %copy-done.23, bf16[528,1152]{1,0:T(8,128)(2,1)S(1)} %arrange.1.g_ref, bf16[1152,1152]{1,0:T(8,128)(2,1)} %bitcast.203, ...), custom_call_target="tpu_custom_call" | custom-call | flops 7007109120 | bytes 5308416 | tf_op jit(solution)/shard_map/feed/pallas_call | solution.py:963
  227.9 7.2 %convolution_convert_fusion.4 = bf16[1152,1152]{1,0:T(8,128)(2,1)} fusion(bf16[528,1152]{1,0:T(8,128)(2,1)} %collective-permute-done.8, bf16[528,1152]{1,0:T(8,128)(2,1)S(1)} %copy-done.63, bf16[528,1152]{1,0:T(8,128)(2,1)} %collective-permute-done.9, bf16[528,1152]{1,0:T(8,128)(2,1)S(1)} %arrange.1.g_ref), kind=kOutput, calls=%fused_computation.4 | convolution fusion | flops 2813902848 | bytes 7520256 | tf_op jit(solution)/shard_map/tf,tc->fc/dot_general | solution.py:809
  237.4 5.3 convolution_convert_fusion.3
  242.6 11.4 %feed.6 = (bf16[528,1152]{1,0:T(8,128)(2,1)S(1)}, bf16[528,1152]{1,0:T(8,128)(2,1)S(1)}, f32[1,1152]{1,0:T(1,128)S(1)}, f32[528,1152]{1,0:T(8,128)S(1)}, f32[528,1152]{1,0:T(8,128)S(1)}) custom-call(bf16[528,1152]{1,0:T(8,128)(2,1)S(1)} %copy-done.24, bf16[528,1152]{1,0:T(8,128)(2,1)S(1)} %arrange.1.g_ref, bf16[1152,1152]{1,0:T(8,128)(2,1)} %bitcast.170, ...), custom_call_target="tpu_custom_call" | custom-call | flops 7007109120 | bytes 5308416 | tf_op jit(solution)/shard_map/feed/pallas_call | solution.py:963
  256.8 11.3 %feed.7 = (bf16[528,1152]{1,0:T(8,128)(2,1)}, bf16[528,1152]{1,0:T(8,128)(2,1)}, f32[1,1152]{1,0:T(1,128)S(1)}, f32[528,1152]{1,0:T(8,128)S(1)}, f32[528,1152]{1,0:T(8,128)S(1)}) custom-call(bf16[528,1152]{1,0:T(8,128)(2,1)S(1)} %copy-done.24, bf16[528,1152]{1,0:T(8,128)(2,1)S(1)} %copy-done.6, bf16[1152,1152]{1,0:T(8,128)(2,1)} %bitcast.202, ...), custom_call_target="tpu_custom_call" | custom-call | flops 7007109120 | bytes 5308416 | tf_op jit(solution)/shard_map/feed/pallas_call | solution.py:963
  273.1 3.8 convert_reduce_fusion
  276.9 3.4 convolution_convert_fusion.8
  280.5 19.1 %attend_back.1 = (bf16[2,264,1152]{2,1,0:T(8,128)(2,1)S(1)}, bf16[2,264,1152]{2,1,0:T(8,128)(2,1)S(1)}, bf16[2,264,1152]{2,1,0:T(8,128)(2,1)S(1)}, bf16[2,264,17...) custom-call(bf16[2,264,1152]{2,1,0:T(8,128)(2,1)S(1)} %bitcast.179, bf16[2,264,1152]{2,1,0:T(8,128)(2,1)S(1)} %bitcast.177, ...), custom_call_target="tpu_custom_call" | custom-call | flops 1605795840 | bytes 8515584 | tf_op jit(solution)/shard_map/attend_back/pallas_call | solution.py:918
  313.3 7.6 %convolution_convert_fusion.1 = bf16[1152,1152]{1,0:T(8,128)(2,1)} fusion(bf16[528,1152]{1,0:T(8,128)(2,1)} %collective-permute-done.13, bf16[528,1152]{1,0:T(8,128)(2,1)} %copy-done.61, bf16[528,1152]{1,0:T(8,128)(2,1)} %copy-done.93, bf16[528,1152]{1,0:T(8,128)(2,1)S(1)} %copy-done.25), kind=kOutput, calls=%fused_computation.1 | convolution fusion | flops 2813902848 | bytes 7520256 | tf_op jit(solution)/shard_map/tf,tc->fc/dot_general | solution.py:809
  321.5 7.2 %convolution_convert_fusion.2 = bf16[1152,1152]{1,0:T(8,128)(2,1)} fusion(bf16[528,1152]{1,0:T(8,128)(2,1)} %collective-permute-done.12, bf16[528,1152]{1,0:T(8,128)(2,1)S(1)} %copy-done.60, bf16[528,1152]{1,0:T(8,128)(2,1)} %collective-permute-done.9, bf16[528,1152]{1,0:T(8,128)(2,1)S(1)} %copy-done.7), kind=kOutput, calls=%fused_computation.2 | convolution fusion | flops 2813902848 | bytes 7520256 | tf_op jit(solution)/shard_map/tf,tc->fc/dot_general | solution.py:809
  328.7 5.1 convolution_convert_fusion.7
  338.7 2.6 multiply_reduce_fusion.1
  341.4 3.3 convert_reduce_fusion.2
  344.7 4.8 convolution_convert_fusion.6
  352.5 3.3 add_convert_fusion.1
  366.8 9.0 %convolution_convert_fusion.5 = bf16[1728,1152]{1,0:T(8,128)(2,1)} fusion(bf16[1056,1152]{1,0:T(8,128)(2,1)S(1)} %copy-done.81, bf16[528,1728]{1,0:T(8,128)(2,1)} %collective-permute-done.20, bf16[528,1728]{1,0:T(8,128)(2,1)S(1)} %bitcast.173), kind=kOutput, calls=%fused_computation.5 | convolution fusion | flops 4213555200 | bytes 10063872 | tf_op jit(solution)/shard_map/tf,tc->fc/dot_general | solution.py:809
  375.8 16.4 %collective-permute-done.16 = bf16[576,1152]{1,0:T(8,128)(2,1)} collective-permute-done((bf16[576,1152]{1,0:T(8,128)(2,1)}, bf16[576,1152]{1,0:T(8,128)(2,1)}, u32[]{:S(2)}, u32[]{:S(2)}) %collective-permute-start.16) | collective-permute-done | bytes 1327136 | tf_op jit(solution)/shard_map/ppermute | solution.py:315
  395.9 5.3 convolution_convert_fusion
  401.2 9.3 %collective-permute-done.21 = bf16[288,1152]{1,0:T(8,128)(2,1)S(1)} collective-permute-done((bf16[288,1152]{1,0:T(8,128)(2,1)S(1)}, bf16[288,1152]{1,0:T(8,128)(2,1)S(1)}, u32[]{:S(2)}, u32[]{:S(2)}) %collective-permute-start.21) | collective-permute-done | bytes 663584 | tf_op jit(solution)/shard_map/ppermute | solution.py:315
  411.5 4.0 add_convert_fusion
  415.5 199.6 %reduce_grads.1 = (bf16[12,2,2,24,1152]{4,3,2,1,0:T(8,128)(2,1)}, bf16[3,2,2,24,1152]{4,3,2,1,0:T(8,128)(2,1)}, bf16[3,2,2,24,1152]{4,3,2,1,0:T(8,128)(2,1)}, bf...) custom-call(bf16[12,2,2,24,1152]{4,3,2,1,0:T(8,128)(2,1)} %bitcast.1, ...), custom_call_target="tpu_custom_call" | custom-call | tf_op jit(solution)/shard_map/reduce_grads/pallas_call | solution.py:654
  617.5 2.9 bitcast_convert_fusion
  630.3 4.5 bitcast_convert_fusion.1
  (358 shorter events, 139.4 us)
Async XLA Ops:
  109.0 19.7 %collective-permute-start = (bf16[2,528,288]{1,2,0:T(8,128)(2,1)}, bf16[2,528,288]{1,2,0:T(8,128)(2,1)}, u32[]{:S(2)}, u32[]{:S(2)}) collective-permute-start(bf16[2,528,288]{1,2,0:T(8,128)(2,1)} %bitcast.1), channel_id=1, source_target_pairs={{0,2},{1,3},{2,0},{3,1},{4,6},{5,7},{6,4},{7,5},{8,10},{9,11},{10,... | collective-permute-start | bytes 1824776 | tf_op jit(solution)/shard_map/ppermute | solution.py:315
  117.5 67.5 %collective-permute-start.4 = (bf16[1152,1152]{1,0:T(8,128)(2,1)}, bf16[1152,1152]{1,0:T(8,128)(2,1)}, u32[]{:S(2)}, u32[]{:S(2)}) collective-permute-start(bf16[1152,1152]{1,0:T(8,128)(2,1)} %down_ref.1), channel_id=1, source_target_pairs={{0,2},{1,3},{2,0},{3,1},{4,6},{5,7},{6,4},{7,5},{8,10},{9,11},{10,... | collective-permute-start | bytes 7962632 | tf_op jit(solution)/shard_map/ppermute | solution.py:315
  125.0 21.7 %copy-start.64 = (f32[528,1152]{1,0:T(8,128)}, f32[528,1152]{1,0:T(8,128)S(1)}, u32[]{:S(2)}) copy-start(f32[528,1152]{1,0:T(8,128)S(1)} %convolution_add_fusion.2) | copy-start | bytes 7299076
  129.7 19.1 %collective-permute-start.1 = (bf16[528,1152]{1,0:T(8,128)(2,1)S(1)}, bf16[528,1152]{1,0:T(8,128)(2,1)S(1)}, u32[]{:S(2)}, u32[]{:S(2)}) collective-permute-start(bf16[528,1152]{1,0:T(8,128)(2,1)S(1)} %add_convert_fusion.3), channel_id=1, source_target_pairs={{0,1},{1,0},{2,3},{3,2},{4,5},{5,4},{6,7},{7,6},{8,9},{9,8},{10,11... | collective-permute-start | bytes 3649544 | tf_op jit(solution)/shard_map/ppermute | solution.py:315
  150.9 34.1 %copy-start.14 = (bf16[4,528,288]{2,1,0:T(8,128)(2,1)S(1)}, bf16[4,528,288]{2,1,0:T(8,128)(2,1)}, u32[]{:S(2)}) copy-start(bf16[4,528,288]{2,1,0:T(8,128)(2,1)} %copy-done.13) | copy-start | bytes 3649540
  150.9 35.1 %copy-start.94 = (f32[8]{0:T(128)S(1)}, f32[8]{0:T(128)}, u32[]{:S(2)}) copy-start(f32[8]{0:T(128)} %param.26) | copy-start | bytes 100
  151.0 35.1 %copy-start.95 = (s32[8]{0:T(128)S(1)}, s32[8]{0:T(128)}, u32[]{:S(2)}) copy-start(s32[8]{0:T(128)} %param.25) | copy-start | bytes 100
  185.0 25.5 %collective-permute-start.5 = (bf16[1152,1152]{1,0:T(8,128)(2,1)}, bf16[1152,1152]{1,0:T(8,128)(2,1)}, u32[]{:S(2)}, u32[]{:S(2)}) collective-permute-start(bf16[1152,1152]{1,0:T(8,128)(2,1)} %collective-permute-done.4.down_ref), channel_id=1, source_target_pairs={{0,1},{1,0},{2,3},{3,2},{4,5},{5,4},{6,7},{7,6},{8,9},{9,8},{10,11... | collective-permute-start | bytes 7962632 | tf_op jit(solution)/shard_map/ppermute | solution.py:315
  187.5 3.8 collective-permute-start.2
  193.8 48.9 %copy-start.5 = (bf16[528,1152]{1,0:T(8,128)(2,1)}, bf16[528,1152]{1,0:T(8,128)(2,1)S(1)}, u32[]{:S(2)}) copy-start(bf16[528,1152]{1,0:T(8,128)(2,1)S(1)} %arrange.1.g_ref) | copy-start | bytes 3649540
  193.8 33.9 %collective-permute-start.9 = (bf16[528,1152]{1,0:T(8,128)(2,1)S(1)}, bf16[528,1152]{1,0:T(8,128)(2,1)}, u32[]{:S(2)}, u32[]{:S(2)}) collective-permute-start(bf16[528,1152]{1,0:T(8,128)(2,1)S(1)} %arrange.1.g_ref), channel_id=1, source_target_pairs={{0,1},{1,0},{2,3},{3,2},{4,5},{5,4},{6,7},{7,6},{8,9},{9,8},{10,11... | collective-permute-start | bytes 3649544 | tf_op jit(solution)/shard_map/ppermute | solution.py:315
  210.5 15.7 %copy-start.17 = (bf16[2,264,1152]{2,1,0:T(8,128)(2,1)S(1)}, bf16[2,264,1152]{2,1,0:T(8,128)(2,1)}, u32[]{:S(2)}) copy-start(bf16[2,264,1152]{2,1,0:T(8,128)(2,1)} %copy-done.16) | copy-start | bytes 3649540
  224.7 3.2 collective-permute-start.8
  224.8 10.9 %collective-permute-start.7 = (bf16[528,1152]{1,0:T(8,128)(2,1)}, bf16[528,1152]{1,0:T(8,128)(2,1)}, u32[]{:S(2)}, u32[]{:S(2)}) collective-permute-start(bf16[528,1152]{1,0:T(8,128)(2,1)} %get-tuple-element.132), channel_id=1, source_target_pairs={{0,1},{1,0},{2,3},{3,2},{4,5},{5,4},{6,7},{7,6},{8,9},{9,8},{10,11... | collective-permute-start | bytes 3649544 | tf_op jit(solution)/shard_map/ppermute | solution.py:315
  225.2 29.9 %collective-permute-start.3 = (bf16[1152,1152]{1,0:T(8,128)(2,1)}, bf16[1152,1152]{1,0:T(8,128)(2,1)}, u32[]{:S(2)}, u32[]{:S(2)}) collective-permute-start(bf16[1152,1152]{1,0:T(8,128)(2,1)} %down_ref.1), channel_id=1, source_target_pairs={{0,1},{1,0},{2,3},{3,2},{4,5},{5,4},{6,7},{7,6},{8,9},{9,8},{10,11... | collective-permute-start | bytes 7962632 | tf_op jit(solution)/shard_map/ppermute | solution.py:315
  225.8 11.5 %collective-permute-start.6 = (bf16[528,1152]{1,0:T(8,128)(2,1)}, bf16[528,1152]{1,0:T(8,128)(2,1)S(1)}, u32[]{:S(2)}, u32[]{:S(2)}) collective-permute-start(bf16[528,1152]{1,0:T(8,128)(2,1)} %get-tuple-element.291.n_ref), channel_id=1, source_target_pairs={{0,1},{1,0},{2,3},{3,2},{4,5},{5,4},{6,7},{7,6},{8,9},{9,8},{10,11... | collective-permute-start | bytes 3649544 | tf_op jit(solution)/shard_map/ppermute | solution.py:315
  227.7 101.1 %collective-permute-start.18 = (bf16[528,576]{1,0:T(8,128)(2,1)}, bf16[528,576]{1,0:T(8,128)(2,1)}, u32[]{:S(2)}, u32[]{:S(2)}) collective-permute-start(bf16[528,576]{1,0:T(8,128)(2,1)} %get-tuple-element.306), channel_id=1, source_target_pairs={{0,1},{1,0},{2,3},{3,2},{4,5},{5,4},{6,7},{7,6},{8,9},{9,8},{10,11... | collective-permute-start | bytes 1824776 | tf_op jit(solution)/shard_map/ppermute | solution.py:315
  235.2 98.7 %collective-permute-start.15 = (bf16[1152,1152]{1,0:T(8,128)(2,1)}, bf16[1152,1152]{1,0:T(8,128)(2,1)}, u32[]{:S(2)}, u32[]{:S(2)}) collective-permute-start(bf16[1152,1152]{1,0:T(8,128)(2,1)} %convolution_convert_fusion.4), channel_id=1, source_target_pairs={{0,2},{1,3},{2,0},{3,1},{4,6},{5,7},{6,4},{7,5},{8,10},{9,11},{10,... | collective-permute-start | bytes 7962632 | tf_op jit(solution)/shard_map/ppermute | solution.py:315
  269.2 42.5 %collective-permute-start.13 = (bf16[528,1152]{1,0:T(8,128)(2,1)}, bf16[528,1152]{1,0:T(8,128)(2,1)}, u32[]{:S(2)}, u32[]{:S(2)}) collective-permute-start(bf16[528,1152]{1,0:T(8,128)(2,1)} %get-tuple-element.143), channel_id=1, source_target_pairs={{0,1},{1,0},{2,3},{3,2},{4,5},{5,4},{6,7},{7,6},{8,9},{9,8},{10,11... | collective-permute-start | bytes 3649544 | tf_op jit(solution)/shard_map/ppermute | solution.py:315
  272.6 29.7 %collective-permute-start.10 = (bf16[2,528,288]{1,2,0:T(8,128)(2,1)}, bf16[2,528,288]{1,2,0:T(8,128)(2,1)S(1)}, u32[]{:S(2)}, u32[]{:S(2)}) collective-permute-start(bf16[2,528,288]{1,2,0:T(8,128)(2,1)} %copy.82), channel_id=1, source_target_pairs={{0,1},{1,0},{2,3},{3,2},{4,5},{5,4},{6,7},{7,6},{8,9},{9,8},{10,11... | collective-permute-start | bytes 1824776 | tf_op jit(solution)/shard_map/ppermute | solution.py:315
  280.3 40.6 %collective-permute-start.12 = (bf16[528,1152]{1,0:T(8,128)(2,1)}, bf16[528,1152]{1,0:T(8,128)(2,1)}, u32[]{:S(2)}, u32[]{:S(2)}) collective-permute-start(bf16[528,1152]{1,0:T(8,128)(2,1)} %get-tuple-element.141), channel_id=1, source_target_pairs={{0,1},{1,0},{2,3},{3,2},{4,5},{5,4},{6,7},{7,6},{8,9},{9,8},{10,11... | collective-permute-start | bytes 3649544 | tf_op jit(solution)/shard_map/ppermute | solution.py:315
  280.5 21.7 %copy-start.1 = (bf16[4,528,288]{2,1,0:T(8,128)(2,1)S(1)}, bf16[4,528,288]{2,1,0:T(8,128)(2,1)}, u32[]{:S(2)}) copy-start(bf16[4,528,288]{2,1,0:T(8,128)(2,1)} %copy-done) | copy-start | bytes 3649540
  302.3 26.4 %collective-permute-start.19 = (bf16[528,1152]{1,0:T(8,128)(2,1)}, bf16[528,1152]{1,0:T(8,128)(2,1)}, u32[]{:S(2)}, u32[]{:S(2)}) collective-permute-start(bf16[528,1152]{1,0:T(8,128)(2,1)} %get-tuple-element.279), channel_id=1, source_target_pairs={{0,1},{1,0},{2,3},{3,2},{4,5},{5,4},{6,7},{7,6},{8,9},{9,8},{10,11... | collective-permute-start | bytes 3649544 | tf_op jit(solution)/shard_map/ppermute | solution.py:315
  311.7 89.4 %collective-permute-start.14 = (bf16[1152,1152]{1,0:T(8,128)(2,1)}, bf16[1152,1152]{1,0:T(8,128)(2,1)}, u32[]{:S(2)}, u32[]{:S(2)}) collective-permute-start(bf16[1152,1152]{1,0:T(8,128)(2,1)} %convolution_convert_fusion.3), channel_id=1, source_target_pairs={{0,2},{1,3},{2,0},{3,1},{4,6},{5,7},{6,4},{7,5},{8,10},{9,11},{10,... | collective-permute-start | bytes 7962632 | tf_op jit(solution)/shard_map/ppermute | solution.py:315
  320.9 301.2 %collective-permute-start.11 = (bf16[2,528,288]{1,2,0:T(8,128)(2,1)}, bf16[2,528,288]{1,2,0:T(8,128)(2,1)}, u32[]{:S(2)}, u32[]{:S(2)}) collective-permute-start(bf16[2,528,288]{1,2,0:T(8,128)(2,1)} %copy.85), channel_id=1, source_target_pairs={{0,2},{1,3},{2,0},{3,1},{4,6},{5,7},{6,4},{7,5},{8,10},{9,11},{10,... | collective-permute-start | bytes 1824776 | tf_op jit(solution)/shard_map/ppermute | solution.py:315
  349.5 14.4 %collective-permute-start.17 = (bf16[528,1152]{1,0:T(8,128)(2,1)}, bf16[528,1152]{1,0:T(8,128)(2,1)}, u32[]{:S(2)}, u32[]{:S(2)}) collective-permute-start(bf16[528,1152]{1,0:T(8,128)(2,1)} %get-tuple-element.281), channel_id=1, source_target_pairs={{0,1},{1,0},{2,3},{3,2},{4,5},{5,4},{6,7},{7,6},{8,9},{9,8},{10,11... | collective-permute-start | bytes 3649544 | tf_op jit(solution)/shard_map/ppermute | solution.py:315
  349.5 16.3 %collective-permute-start.20 = (bf16[528,1728]{1,0:T(8,128)(2,1)S(1)}, bf16[528,1728]{1,0:T(8,128)(2,1)}, u32[]{:S(2)}, u32[]{:S(2)}) collective-permute-start(bf16[528,1728]{1,0:T(8,128)(2,1)S(1)} %bitcast.172), channel_id=1, source_target_pairs={{0,1},{1,0},{2,3},{3,2},{4,5},{5,4},{6,7},{7,6},{8,9},{9,8},{10,11... | collective-permute-start | bytes 5474312 | tf_op jit(solution)/shard_map/ppermute | solution.py:315
  352.3 8.0 %collective-permute-start.22 = (f32[9,1152]{1,0:T(8,128)S(1)}, f32[9,1152]{1,0:T(8,128)S(1)}, u32[]{:S(2)}, u32[]{:S(2)}) collective-permute-start(f32[9,1152]{1,0:T(8,128)S(1)} %concatenate.129), channel_id=1, source_target_pairs={{0,1},{1,0},{2,3},{3,2},{4,5},{5,4},{6,7},{7,6},{8,9},{9,8},{10,11... | collective-permute-start | bytes 124424 | tf_op jit(solution)/shard_map/ppermute | solution.py:315
  360.3 31.8 %collective-permute-start.16 = (bf16[576,1152]{1,0:T(8,128)(2,1)}, bf16[576,1152]{1,0:T(8,128)(2,1)}, u32[]{:S(2)}, u32[]{:S(2)}) collective-permute-start(bf16[576,1152]{1,0:T(8,128)(2,1)} %dynamic-slice_bitcast_fusion), channel_id=1, source_target_pairs={{0,4},{4,0},{8,12},{12,8},{16,20},{20,16},{24,28},{28,24},{1,5},{5... | collective-permute-start | bytes 3981320 | tf_op jit(solution)/shard_map/ppermute | solution.py:315
  365.8 26.3 %copy-start.69 = (bf16[1152,1152]{1,0:T(8,128)(2,1)S(1)}, bf16[1152,1152]{1,0:T(8,128)(2,1)}, u32[]{:S(2)}) copy-start(bf16[1152,1152]{1,0:T(8,128)(2,1)} %copy-done.68) | copy-start | bytes 7962628
  394.0 16.4 %collective-permute-start.21 = (bf16[288,1152]{1,0:T(8,128)(2,1)S(1)}, bf16[288,1152]{1,0:T(8,128)(2,1)S(1)}, u32[]{:S(2)}, u32[]{:S(2)}) collective-permute-start(bf16[288,1152]{1,0:T(8,128)(2,1)S(1)} %dynamic-slice_bitcast_fusion.5), channel_id=1, source_target_pairs={{0,8},{4,12},{8,0},{12,4},{16,24},{20,28},{24,16},{28,20},{1,9},{5... | collective-permute-start | bytes 1990664 | tf_op jit(solution)/shard_map/ppermute | solution.py:315
  395.9 15.6 %copy-start.79 = (bf16[1152,1152]{1,0:T(8,128)(2,1)S(1)}, bf16[1152,1152]{1,0:T(8,128)(2,1)}, u32[]{:S(2)}) copy-start(bf16[1152,1152]{1,0:T(8,128)(2,1)} %convolution_convert_fusion.1) | copy-start | bytes 7962628
  (89 other events, 324.0 us)
where the time goes:
time: 654 us; the launch traced here: 644 us
  Pallas kernels  352 us (54%)
  local copies, waits for them, and re-layouts  94.7 us (14%)
  matrix products  75.5 us (12%)
  waiting for transfers between devices  61.2 us (9%)
  other arithmetic  48 us (7%)
  starting transfers between devices  10.7 us (2%)
    pallas_call x1, Pallas kernels, reduce_grads(): pl.pallas_call(functools.partial(reduce_kernel, sizes, views, len(arrays)...  200 us
    dot_general x17, matrix products, dot(): return jnp.einsum(spec, left, right, preferred_element_type=jnp.float32)  75.5 us
    pallas_call x1, Pallas kernels, gather_weights(): pl.pallas_call(functools.partial(gather_kernel, pieces, len(arrays), len(...  74.2 us
    ppermute x23, waiting for transfers between devices, swap(): lax.ppermute(value, axis, [(i, i ^ bit) for i in range(lax.axis_size(axis...  61.2 us
    unnamed x206, local copies, waits for them, and re-layouts  58.8 us
    pallas_call x4, Pallas kernels, feed(): pl.pallas_call(functools.partial(feed_kernel, d_n is None), grid=(hidden...  45.2 us
    pallas_call x1, Pallas kernels, attention_back(): pl.pallas_call(attend_back_kernel, out_shape=[shape(cols)] * 3 + [shape(3...  19.1 us
  transfers between devices with their start and end apart: 23, of which 6 were waited for; matrix products, arithmetic and copies ran while one was open for 22% of the time, Pallas kernels for 43%

commit v1 on v0

--- a/solution.py
+++ b/solution.py
@@ -1110,30 +1110,30 @@
 
     result, d_n2 = stream_two + b_down_all, None
     acts, d_up, g_b_up = [None] * 4, [None] * 4, [None] * 4
-    wd_y, stream_two_then = meet(wd_y, result)
-    result = stream_two_then
-    wd = [w_down, wd_y, wd_core, other(wd_y)]
+    wd = [w_down, None, wd_core, None]
 
     def run_feed(r, result, d_n2):
         bias = b_up_all[:, r * width : (r + 1) * width]
         acts[r], d_up[r], g_b_up[r], result, d_n2 = feed(full_two, grad_low, wu[r], bias, wd[r], result, d_n2)
         return result, d_n2
 
-    for r in (1, 3):
+    for r in (0, 2, 1, 3):
+        if r == 1:
+            wd_y, d_n2 = meet(wd_y, d_n2)
+            wd[1], wd[3] = wd_y, other(wd_y)
         result, d_n2 = run_feed(r, result, d_n2)
     down_theirs = weight_grad(both(acts[1], other(acts[3])), grad_both)
     down_come = swap(down_theirs, ACROSS_Y)
     up_theirs = weight_grad(n2_both, after(both(d_up[1], other(d_up[3])), down_theirs))
     up_come = swap(up_theirs, ACROSS_Y)
-    d_n2, up_theirs = meet(d_n2, up_theirs)
-    result, d_n2 = run_feed(0, result, d_n2)
-    result, d_n2 = run_feed(2, result, d_n2)
+    d_n2, result, acts[0], d_up[0], up_theirs = meet(d_n2, result, acts[0], d_up[0], up_theirs)
     g_b_up = jnp.concatenate(g_b_up)
     down_mine = weight_grad(both(acts[0], other(acts[2])), grad_both)
     up_mine = weight_grad(n2_both, both(d_up[0], other(d_up[2])))
     down_mine, up_mine = meet(down_mine, up_mine)
 
     outs = disperse(result, row_valid)
+    d_n2 = after(d_n2, outs)
     out_core = other(outs[2:])
     out_y = swap(after(jnp.stack([outs[1], out_core[1]]), up_theirs), ACROSS_Y)
     back_two, g_ln2_gain, g_ln2_bias = norm_rows_back(d_n2, normed_two, rstd_two, gain_two)
@@ -1144,11 +1144,7 @@
     proj_part = chunked(weight_grad(attended_both, both(d_stream_two, other(d_stream_two))), (2,))
     d_attended = low(dot("tc,fc->tf", d_stream_two, wp))
     d_qkv = attention_back(query, key, value, logsum, d_attended)
-    down_come, *d_qkv = meet(down_come, *d_qkv)
-    down_keep, down_send = split(add_low(down_mine, down_come), x)
-    down_come = swap(down_send, ACROSS_X)
     *d_qkv, d_own, d_partner = d_qkv
-    qkv_part = chunked(weight_grad(both(d_own, other(d_partner)), n1_both), (3, 2))
     d_n1 = sum(dot("tc,cd->td", d, w) for d, w in zip(d_qkv, (wq, wk, wv)))
     back_one, g_ln1_gain, g_ln1_bias = norm_rows_back(d_n1, normed_one, rstd_one, gain_one)
     d_stream = low(back_one + d_stream_wide)
@@ -1156,13 +1152,15 @@
     g_b_skip = jnp.sum(d_stream.astype(jnp.float32), 0)
     d_skip = low(dot("tc,fc->tf", d_stream, wskip))
     d_blocks = jnp.stack(jnp.split(d_skip, 4, 1))
-    down_come, d_stream_both, d_blocks, proj_part, qkv_part = meet(
-        down_come, d_stream_both, d_blocks, proj_part, qkv_part
-    )
+    down_come, d_blocks, proj_part, n1_both = meet(down_come, d_blocks, proj_part, n1_both)
+    down_keep, down_send = split(add_low(down_mine, down_come), x)
+    down_come = swap(down_send, ACROSS_X)
+    qkv_part = chunked(weight_grad(both(d_own, other(d_partner)), n1_both), (3, 2))
+    skip_part = chunked(weight_grad(skip_both, d_stream_both), (2,))
+    down_come, skip_part, qkv_part = meet(down_come, skip_part, qkv_part)
     down_keep, down_send = split(add_low(down_keep, down_come), z)
     down_come = swap(down_send, ACROSS_Z)
-    skip_part = chunked(weight_grad(skip_both, d_stream_both), (2,))
-    up_come, down_come, skip_part = meet(up_come, down_come, skip_part)
+    up_come, skip_part = meet(up_come, skip_part)
     down_quarter = add_low(down_keep, down_come)
     ready = chunked(add_low(up_mine, up_come), ())
 

time: 654 us -> 681 us (1.041)
  waiting for transfers between devices: 61.2 us -> 88.8 us
  matrix products: 75.5 us -> 86 us
  local copies, waits for them, and re-layouts: 94.7 us -> 86.5 us
    ppermute x23, waiting for transfers between devices: 61.2 us -> 88.8 us  [swap(): lax.ppermute(value, axis, [(i, i ^ bit) for i in range(lax.axis_size(axis...]
    dot_general x17, matrix products: 75.5 us -> 86 us  [dot(): return jnp.einsum(spec, left, right, preferred_element_type=jnp.float32)]
    unnamed x206 -> x176, local copies, waits for them, and re-layouts: 58.8 us -> 52.1 us
  transfers between devices with their start and end apart: 23 -> 23, of which waited for: 6 -> 3; matrix products, arithmetic and copies ran while one was open for 22% -> 21% of each run, Pallas kernels for 43% -> 41%
where the time goes in v1:
time: 681 us; the launch traced here: 676 us
  Pallas kernels  357 us (52%)
  waiting for transfers between devices  88.8 us (13%)
  local copies, waits for them, and re-layouts  86.5 us (13%)
  matrix products  86 us (13%)
  other arithmetic  44.3 us (7%)
  starting transfers between devices  11.4 us (2%)
    pallas_call x1, Pallas kernels, reduce_grads(): pl.pallas_call(functools.partial(reduce_kernel, sizes, views, len(arrays)...  200 us
    ppermute x23, waiting for transfers between devices, swap(): lax.ppermute(value, axis, [(i, i ^ bit) for i in range(lax.axis_size(axis...  88.8 us
    dot_general x17, matrix products, dot(): return jnp.einsum(spec, left, right, preferred_element_type=jnp.float32)  86 us
    pallas_call x1, Pallas kernels, gather_weights(): pl.pallas_call(functools.partial(gather_kernel, pieces, len(arrays), len(...  74.2 us
    unnamed x176, local copies, waits for them, and re-layouts  52.1 us
    pallas_call x4, Pallas kernels, feed(): pl.pallas_call(functools.partial(feed_kernel, d_n is None), grid=(hidden...  48.1 us
    pallas_call x1, Pallas kernels, attention_back(): pl.pallas_call(attend_back_kernel, out_shape=[shape(cols)] * 3 + [shape(3...  20.4 us
  transfers between devices with their start and end apart: 23, of which 3 were waited for; matrix products, arithmetic and copies ran while one was open for 21% of the time, Pallas kernels for 41%

profile of v1, /device:TPU:0, one launch (start us, length us, event | category | flops | bytes accessed | tf_op | source)
XLA Modules:
  0.0 676.5 jit_solution(4341063582141659505)
XLA Ops:
  24.0 74.2 %gather_weights.1 = (bf16[2,528,576]{2,1,0:T(8,128)(2,1)S(1)}, bf16[528,576]{1,0:T(8,128)(2,1)S(1)}, bf16[528,576]{1,0:T(8,128)(2,1)S(1)}, f32[11,288]{1,0:T(8,1...) custom-call(bf16[2,2,528,576]{3,2,1,0:T(8,128)(2,1)} %bitcast.148, ...), custom_call_target="tpu_custom_call" | custom-call | tf_op jit(solution)/shard_map/gather_weights/pallas_call | solution.py:454
  112.6 6.2 concatenate.112
  122.9 8.1 %convolution_add_fusion.3 = f32[528,1152]{1,0:T(8,128)} fusion(bf16[528,2304]{1,0:T(8,128)(2,1)} %concatenate.112, bf16[2304,1152]{1,0:T(8,128)(2,1)} %bitcast.196, f32[1152]{0:T(1024)S(1)} %get-tuple-element.273), kind=kOutput, calls=%fused_computation.15 | convolution fusion | flops 2803451904 | bytes 10179072 | tf_op jit(solution)/shard_map/td,dc->tc/dot_general | solution.py:809
  132.6 3.6 fusion.7
  136.1 58.8 %collective-permute-done = bf16[2,528,288]{1,2,0:T(8,128)(2,1)} collective-permute-done((bf16[2,528,288]{1,2,0:T(8,128)(2,1)}, bf16[2,528,288]{1,2,0:T(8,128)(2,1)}, u32[]{:S(2)}, u32[]{:S(2)}) %collective-permute-start) | collective-permute-done | bytes 608288 | tf_op jit(solution)/shard_map/ppermute | solution.py:315
  199.7 3.4 convolution_convert_fusion.9
  203.1 3.7 convolution_convert_fusion.10
  206.9 3.7 convolution_convert_fusion.11
  210.6 9.6 %attend.1 = (bf16[2,264,1152]{2,1,0:T(8,128)(2,1)S(1)}, f32[2,16,264]{2,1,0:T(8,128)S(1)}) custom-call(bf16[2,264,1152]{2,1,0:T(8,128)(2,1)S(1)} %bitcast.175, bf16[2,264,1152]{2,1,0:T(8,128)(2,1)S(1)} %bitcast.173, bf16[2,264,1152]{2,1,0:T(8,128)(2,1)S(1)} %bitcast.171), custom_call_target="tpu_custom_call" | custom-call | flops 642318336 | bytes 4866048 | tf_op jit(solution)/shard_map/attend/pallas_call | solution.py:899
  220.3 3.4 fusion.3
  226.2 3.4 pad_maximum_fusion.4
  230.6 12.1 %feed.4 = (bf16[528,1152]{1,0:T(8,128)(2,1)S(1)}, bf16[528,1152]{1,0:T(8,128)(2,1)S(1)}, f32[1,1152]{1,0:T(1,128)S(1)}, f32[528,1152]{1,0:T(8,128)S(1)}, f32[528,1152]{1,0:T(8,128)S(1)}) custom-call(bf16[528,1152]{1,0:T(8,128)(2,1)S(1)} %get-tuple-element.289.n_ref, bf16[528,1152]{1,0:T(8,128)(2,1)} %arrange.1.g_ref, bf16[1152,1152]{1,0:T(8,128)(2,1)} %bitcast.169, ...), custom_call_target="tpu_custom_call" | custom-call | flops 7007109120 | bytes 5308416 | tf_op jit(solution)/shard_map/feed/pallas_call | solution.py:963
  242.8 12.4 %feed.5 = (bf16[528,1152]{1,0:T(8,128)(2,1)}, bf16[528,1152]{1,0:T(8,128)(2,1)}, f32[1,1152]{1,0:T(1,128)S(1)}, f32[528,1152]{1,0:T(8,128)S(1)}, f32[528,1152]{1,0:T(8,128)S(1)}) custom-call(bf16[528,1152]{1,0:T(8,128)(2,1)S(1)} %get-tuple-element.289.n_ref, bf16[528,1152]{1,0:T(8,128)(2,1)} %arrange.1.g_ref, bf16[1152,1152]{1,0:T(8,128)(2,1)} %bitcast.201, ...), custom_call_target="tpu_custom_call" | custom-call | flops 7007109120 | bytes 5308416 | tf_op jit(solution)/shard_map/feed/pallas_call | solution.py:963
  262.2 11.7 %feed.6 = (bf16[528,1152]{1,0:T(8,128)(2,1)S(1)}, bf16[528,1152]{1,0:T(8,128)(2,1)S(1)}, f32[1,1152]{1,0:T(1,128)S(1)}, f32[528,1152]{1,0:T(8,128)S(1)}, f32[528,1152]{1,0:T(8,128)S(1)}) custom-call(bf16[528,1152]{1,0:T(8,128)(2,1)S(1)} %get-tuple-element.289.n_ref, bf16[528,1152]{1,0:T(8,128)(2,1)} %arrange.1.g_ref, bf16[1152,1152]{1,0:T(8,128)(2,1)} %bitcast.168, ...), custom_call_target="tpu_custom_call" | custom-call | flops 7007109120 | bytes 5308416 | tf_op jit(solution)/shard_map/feed/pallas_call | solution.py:963
  277.2 11.9 %feed.7 = (bf16[528,1152]{1,0:T(8,128)(2,1)}, bf16[528,1152]{1,0:T(8,128)(2,1)}, f32[1,1152]{1,0:T(1,128)S(1)}, f32[528,1152]{1,0:T(8,128)S(1)}, f32[528,1152]{1,0:T(8,128)S(1)}) custom-call(bf16[528,1152]{1,0:T(8,128)(2,1)S(1)} %copy-done.16, bf16[528,1152]{1,0:T(8,128)(2,1)} %arrange.1.g_ref, bf16[1152,1152]{1,0:T(8,128)(2,1)} %bitcast.200, ...), custom_call_target="tpu_custom_call" | custom-call | flops 7007109120 | bytes 5308416 | tf_op jit(solution)/shard_map/feed/pallas_call | solution.py:963
  295.3 7.6 %convolution_convert_fusion.4 = bf16[1152,1152]{1,0:T(8,128)(2,1)} fusion(bf16[528,1152]{1,0:T(8,128)(2,1)} %collective-permute-done.8, bf16[528,1152]{1,0:T(8,128)(2,1)S(1)} %copy-done.51, bf16[528,1152]{1,0:T(8,128)(2,1)} %collective-permute-done.9, bf16[528,1152]{1,0:T(8,128)(2,1)} %arrange.1.g_ref), kind=kOutput, calls=%fused_computation.4 | convolution fusion | flops 2813902848 | bytes 7520256 | tf_op jit(solution)/shard_map/tf,tc->fc/dot_general | solution.py:809
  304.6 5.3 convolution_convert_fusion.3
  312.7 3.4 convert_reduce_fusion
  316.6 3.5 convolution_convert_fusion.8
  320.6 20.4 %attend_back.1 = (bf16[2,264,1152]{2,1,0:T(8,128)(2,1)S(1)}, bf16[2,264,1152]{2,1,0:T(8,128)(2,1)S(1)}, bf16[2,264,1152]{2,1,0:T(8,128)(2,1)S(1)}, bf16[2,264,17...) custom-call(bf16[2,264,1152]{2,1,0:T(8,128)(2,1)S(1)} %bitcast.176, bf16[2,264,1152]{2,1,0:T(8,128)(2,1)S(1)} %bitcast.174, ...), custom_call_target="tpu_custom_call" | custom-call | flops 1605795840 | bytes 8515584 | tf_op jit(solution)/shard_map/attend_back/pallas_call | solution.py:918
  348.4 3.3 convert_reduce_fusion.2
  351.8 6.4 convolution_convert_fusion.6
  361.3 7.1 %convolution_convert_fusion.1 = bf16[1152,1152]{1,0:T(8,128)(2,1)} fusion(bf16[528,1152]{1,0:T(8,128)(2,1)} %collective-permute-done.13, bf16[528,1152]{1,0:T(8,128)(2,1)S(1)} %copy-done.55, bf16[528,1152]{1,0:T(8,128)(2,1)S(1)} %copy-done.78, bf16[528,1152]{1,0:T(8,128)(2,1)S(1)} %copy-done.18), kind=kOutput, calls=%fused_computation.1 | convolution fusion | flops 2813902848 | bytes 7520256 | tf_op jit(solution)/shard_map/tf,tc->fc/dot_general | solution.py:809
  368.7 7.5 %convolution_convert_fusion.2 = bf16[1152,1152]{1,0:T(8,128)(2,1)} fusion(bf16[528,1152]{1,0:T(8,128)(2,1)} %collective-permute-done.12, bf16[528,1152]{1,0:T(8,128)(2,1)S(1)} %copy-done.53, bf16[528,1152]{1,0:T(8,128)(2,1)} %collective-permute-done.9, bf16[528,1152]{1,0:T(8,128)(2,1)} %arrange.1.g_ref), kind=kOutput, calls=%fused_computation.2 | convolution fusion | flops 2813902848 | bytes 7520256 | tf_op jit(solution)/shard_map/tf,tc->fc/dot_general | solution.py:809
  384.8 5.1 convolution_convert_fusion.7
  394.2 7.2 %convolution_convert_fusion = bf16[1152,1152]{1,0:T(8,128)(2,1)} fusion(bf16[1056,1152]{1,0:T(8,128)(2,1)S(1)} %copy-done.65, bf16[528,1152]{1,0:T(8,128)(2,1)} %collective-permute-done.19, bf16[528,1152]{1,0:T(8,128)(2,1)} %get-tuple-element.279), kind=kOutput, calls=%fused_computation | convolution fusion | flops 2809036800 | bytes 7520256 | tf_op jit(solution)/shard_map/tf,tc->fc/dot_general | solution.py:809
  402.6 7.8 %convolution_convert_fusion.5 = bf16[1728,1152]{1,0:T(8,128)(2,1)} fusion(bf16[1056,1152]{1,0:T(8,128)(2,1)S(1)} %copy-done.66, bf16[528,1728]{1,0:T(8,128)(2,1)S(1)} %collective-permute-done.20, bf16[528,1728]{1,0:T(8,128)(2,1)S(1)} %bitcast.170), kind=kOutput, calls=%fused_computation.5 | convolution fusion | flops 4213555200 | bytes 10063872 | tf_op jit(solution)/shard_map/tf,tc->fc/dot_general | solution.py:809
  410.4 13.5 %collective-permute-done.18 = bf16[576,1152]{1,0:T(8,128)(2,1)S(1)} collective-permute-done((bf16[576,1152]{1,0:T(8,128)(2,1)S(1)}, bf16[576,1152]{1,0:T(8,128)(2,1)S(1)}, u32[]{:S(2)}, u32[]{:S(2)}) %collective-permute-start.18) | collective-permute-done | bytes 1327136 | tf_op jit(solution)/shard_map/ppermute | solution.py:315
  425.0 16.5 %collective-permute-done.14 = bf16[1152,1152]{1,0:T(8,128)(2,1)} collective-permute-done((bf16[1152,1152]{1,0:T(8,128)(2,1)}, bf16[1152,1152]{1,0:T(8,128)(2,1)}, u32[]{:S(2)}, u32[]{:S(2)}) %collective-permute-start.14) | collective-permute-done | bytes 2654240 | tf_op jit(solution)/shard_map/ppermute | solution.py:315
  441.5 4.0 add_convert_fusion
  446.5 199.6 %reduce_grads.1 = (bf16[12,2,2,24,1152]{4,3,2,1,0:T(8,128)(2,1)}, bf16[3,2,2,24,1152]{4,3,2,1,0:T(8,128)(2,1)}, bf16[3,2,2,24,1152]{4,3,2,1,0:T(8,128)(2,1)}, bf...) custom-call(bf16[12,2,2,24,1152]{4,3,2,1,0:T(8,128)(2,1)} %bitcast.1, ...), custom_call_target="tpu_custom_call" | custom-call | tf_op jit(solution)/shard_map/reduce_grads/pallas_call | solution.py:654
  662.4 4.5 bitcast_convert_fusion.1
  (328 shorter events, 125.1 us)
Async XLA Ops:
  118.8 124.0 %collective-permute-start.4 = (bf16[1152,1152]{1,0:T(8,128)(2,1)}, bf16[1152,1152]{1,0:T(8,128)(2,1)}, u32[]{:S(2)}, u32[]{:S(2)}) collective-permute-start(bf16[1152,1152]{1,0:T(8,128)(2,1)} %down_ref.1), channel_id=1, source_target_pairs={{0,1},{1,0},{2,3},{3,2},{4,5},{5,4},{6,7},{7,6},{8,9},{9,8},{10,11... | collective-permute-start | bytes 7962632 | tf_op jit(solution)/shard_map/ppermute | solution.py:315
  119.1 138.9 %collective-permute-start.3 = (bf16[1152,1152]{1,0:T(8,128)(2,1)}, bf16[1152,1152]{1,0:T(8,128)(2,1)}, u32[]{:S(2)}, u32[]{:S(2)}) collective-permute-start(bf16[1152,1152]{1,0:T(8,128)(2,1)} %down_ref.1), channel_id=1, source_target_pairs={{0,2},{1,3},{2,0},{3,1},{4,6},{5,7},{6,4},{7,5},{8,10},{9,11},{10,... | collective-permute-start | bytes 7962632 | tf_op jit(solution)/shard_map/ppermute | solution.py:315
  120.9 74.0 %collective-permute-start = (bf16[2,528,288]{1,2,0:T(8,128)(2,1)}, bf16[2,528,288]{1,2,0:T(8,128)(2,1)}, u32[]{:S(2)}, u32[]{:S(2)}) collective-permute-start(bf16[2,528,288]{1,2,0:T(8,128)(2,1)} %bitcast.1), channel_id=1, source_target_pairs={{0,2},{1,3},{2,0},{3,1},{4,6},{5,7},{6,4},{7,5},{8,10},{9,11},{10,... | collective-permute-start | bytes 1824776 | tf_op jit(solution)/shard_map/ppermute | solution.py:315
  136.1 60.9 %copy-start.58 = (f32[528,1152]{1,0:T(8,128)S(1)}, f32[528,1152]{1,0:T(8,128)}, u32[]{:S(2)}) copy-start(f32[528,1152]{1,0:T(8,128)} %convolution_add_fusion.3) | copy-start | bytes 7299076
  197.1 26.8 %collective-permute-start.2 = (bf16[2,528,288]{1,2,0:T(8,128)(2,1)}, bf16[2,528,288]{1,2,0:T(8,128)(2,1)S(1)}, u32[]{:S(2)}, u32[]{:S(2)}) collective-permute-start(bf16[2,528,288]{1,2,0:T(8,128)(2,1)} %pad_maximum_fusion.15), channel_id=1, source_target_pairs={{0,1},{1,0},{2,3},{3,2},{4,5},{5,4},{6,7},{7,6},{8,9},{9,8},{10,11... | collective-permute-start | bytes 1824776 | tf_op jit(solution)/shard_map/ppermute | solution.py:315
  199.0 27.2 %collective-permute-start.1 = (bf16[528,1152]{1,0:T(8,128)(2,1)}, bf16[528,1152]{1,0:T(8,128)(2,1)}, u32[]{:S(2)}, u32[]{:S(2)}) collective-permute-start(bf16[528,1152]{1,0:T(8,128)(2,1)} %add_convert_fusion.3), channel_id=1, source_target_pairs={{0,1},{1,0},{2,3},{3,2},{4,5},{5,4},{6,7},{7,6},{8,9},{9,8},{10,11... | collective-permute-start | bytes 3649544 | tf_op jit(solution)/shard_map/ppermute | solution.py:315
  210.5 13.1 %copy-start.44 = (bf16[528,1152]{1,0:T(8,128)(2,1)}, bf16[528,1152]{1,0:T(8,128)(2,1)S(1)}, u32[]{:S(2)}) copy-start(bf16[528,1152]{1,0:T(8,128)(2,1)S(1)} %convolution_convert_fusion.11) | copy-start | bytes 3649540
  230.6 28.2 %copy-start.15 = (bf16[528,1152]{1,0:T(8,128)(2,1)}, bf16[528,1152]{1,0:T(8,128)(2,1)S(1)}, u32[]{:S(2)}) copy-start(bf16[528,1152]{1,0:T(8,128)(2,1)S(1)} %get-tuple-element.289.n_ref) | copy-start | bytes 3649540
  242.8 12.4 %copy-start.52 = (bf16[528,1152]{1,0:T(8,128)(2,1)}, bf16[528,1152]{1,0:T(8,128)(2,1)S(1)}, u32[]{:S(2)}) copy-start(bf16[528,1152]{1,0:T(8,128)(2,1)S(1)} %get-tuple-element.142) | copy-start | bytes 3649540
  242.8 12.4 %copy-start.54 = (bf16[528,1152]{1,0:T(8,128)(2,1)}, bf16[528,1152]{1,0:T(8,128)(2,1)S(1)}, u32[]{:S(2)}) copy-start(bf16[528,1152]{1,0:T(8,128)(2,1)S(1)} %get-tuple-element.144) | copy-start | bytes 3649540
  258.1 17.9 %collective-permute-start.5 = (bf16[1152,1152]{1,0:T(8,128)(2,1)}, bf16[1152,1152]{1,0:T(8,128)(2,1)}, u32[]{:S(2)}, u32[]{:S(2)}) collective-permute-start(bf16[1152,1152]{1,0:T(8,128)(2,1)} %collective-permute-done.3.down_ref), channel_id=1, source_target_pairs={{0,1},{1,0},{2,3},{3,2},{4,5},{5,4},{6,7},{7,6},{8,9},{9,8},{10,11... | collective-permute-start | bytes 7962632 | tf_op jit(solution)/shard_map/ppermute | solution.py:315
  258.7 36.1 %collective-permute-start.9 = (bf16[528,1152]{1,0:T(8,128)(2,1)}, bf16[528,1152]{1,0:T(8,128)(2,1)}, u32[]{:S(2)}, u32[]{:S(2)}) collective-permute-start(bf16[528,1152]{1,0:T(8,128)(2,1)} %arrange.1.g_ref), channel_id=1, source_target_pairs={{0,1},{1,0},{2,3},{3,2},{4,5},{5,4},{6,7},{7,6},{8,9},{9,8},{10,11... | collective-permute-start | bytes 3649544 | tf_op jit(solution)/shard_map/ppermute | solution.py:315
  290.6 4.7 collective-permute-start.8
  291.1 11.9 %collective-permute-start.7 = (bf16[528,1152]{1,0:T(8,128)(2,1)}, bf16[528,1152]{1,0:T(8,128)(2,1)}, u32[]{:S(2)}, u32[]{:S(2)}) collective-permute-start(bf16[528,1152]{1,0:T(8,128)(2,1)} %get-tuple-element.137), channel_id=1, source_target_pairs={{0,1},{1,0},{2,3},{3,2},{4,5},{5,4},{6,7},{7,6},{8,9},{9,8},{10,11... | collective-permute-start | bytes 3649544 | tf_op jit(solution)/shard_map/ppermute | solution.py:315
  291.4 13.1 %collective-permute-start.6 = (bf16[528,1152]{1,0:T(8,128)(2,1)}, bf16[528,1152]{1,0:T(8,128)(2,1)S(1)}, u32[]{:S(2)}, u32[]{:S(2)}) collective-permute-start(bf16[528,1152]{1,0:T(8,128)(2,1)} %copy-done.15), channel_id=1, source_target_pairs={{0,1},{1,0},{2,3},{3,2},{4,5},{5,4},{6,7},{7,6},{8,9},{9,8},{10,11... | collective-permute-start | bytes 3649544 | tf_op jit(solution)/shard_map/ppermute | solution.py:315
  294.7 89.4 %collective-permute-start.16 = (bf16[528,576]{1,0:T(8,128)(2,1)}, bf16[528,576]{1,0:T(8,128)(2,1)}, u32[]{:S(2)}, u32[]{:S(2)}) collective-permute-start(bf16[528,576]{1,0:T(8,128)(2,1)} %get-tuple-element.304), channel_id=1, source_target_pairs={{0,1},{1,0},{2,3},{3,2},{4,5},{5,4},{6,7},{7,6},{8,9},{9,8},{10,11... | collective-permute-start | bytes 1824776 | tf_op jit(solution)/shard_map/ppermute | solution.py:315
  294.8 66.2 %collective-permute-start.13 = (bf16[528,1152]{1,0:T(8,128)(2,1)}, bf16[528,1152]{1,0:T(8,128)(2,1)}, u32[]{:S(2)}, u32[]{:S(2)}) collective-permute-start(bf16[528,1152]{1,0:T(8,128)(2,1)} %get-tuple-element.145), channel_id=1, source_target_pairs={{0,1},{1,0},{2,3},{3,2},{4,5},{5,4},{6,7},{7,6},{8,9},{9,8},{10,11... | collective-permute-start | bytes 3649544 | tf_op jit(solution)/shard_map/ppermute | solution.py:315
  295.2 73.1 %collective-permute-start.12 = (bf16[528,1152]{1,0:T(8,128)(2,1)}, bf16[528,1152]{1,0:T(8,128)(2,1)}, u32[]{:S(2)}, u32[]{:S(2)}) collective-permute-start(bf16[528,1152]{1,0:T(8,128)(2,1)} %get-tuple-element.143), channel_id=1, source_target_pairs={{0,1},{1,0},{2,3},{3,2},{4,5},{5,4},{6,7},{7,6},{8,9},{9,8},{10,11... | collective-permute-start | bytes 3649544 | tf_op jit(solution)/shard_map/ppermute | solution.py:315
  316.1 68.1 %collective-permute-start.17 = (bf16[528,1152]{1,0:T(8,128)(2,1)}, bf16[528,1152]{1,0:T(8,128)(2,1)}, u32[]{:S(2)}, u32[]{:S(2)}) collective-permute-start(bf16[528,1152]{1,0:T(8,128)(2,1)} %get-tuple-element.277), channel_id=1, source_target_pairs={{0,1},{1,0},{2,3},{3,2},{4,5},{5,4},{6,7},{7,6},{8,9},{9,8},{10,11... | collective-permute-start | bytes 3649544 | tf_op jit(solution)/shard_map/ppermute | solution.py:315
  320.0 69.9 %collective-permute-start.15 = (bf16[1152,1152]{1,0:T(8,128)(2,1)}, bf16[1152,1152]{1,0:T(8,128)(2,1)}, u32[]{:S(2)}, u32[]{:S(2)}) collective-permute-start(bf16[1152,1152]{1,0:T(8,128)(2,1)} %convolution_convert_fusion.4), channel_id=1, source_target_pairs={{0,2},{1,3},{2,0},{3,1},{4,6},{5,7},{6,4},{7,5},{8,10},{9,11},{10,... | collective-permute-start | bytes 7962632 | tf_op jit(solution)/shard_map/ppermute | solution.py:315
  320.6 20.4 %copy-start.32 = (bf16[4,2,2,72,1152]{4,3,2,1,0:T(8,128)(2,1)S(1)}, bf16[4,2,2,72,1152]{4,3,2,1,0:T(8,128)(2,1)}, u32[]{:S(2)}) copy-start(bf16[4,2,2,72,1152]{4,3,2,1,0:T(8,128)(2,1)} %copy-done.30) | copy-start | bytes 7962628
  361.1 33.1 %collective-permute-start.19 = (bf16[528,1152]{1,0:T(8,128)(2,1)}, bf16[528,1152]{1,0:T(8,128)(2,1)}, u32[]{:S(2)}, u32[]{:S(2)}) collective-permute-start(bf16[528,1152]{1,0:T(8,128)(2,1)} %get-tuple-element.279), channel_id=1, source_target_pairs={{0,1},{1,0},{2,3},{3,2},{4,5},{5,4},{6,7},{7,6},{8,9},{9,8},{10,11... | collective-permute-start | bytes 3649544 | tf_op jit(solution)/shard_map/ppermute | solution.py:315
  368.4 10.1 %collective-permute-start.21 = (f32[9,1152]{1,0:T(8,128)S(1)}, f32[9,1152]{1,0:T(8,128)S(1)}, u32[]{:S(2)}, u32[]{:S(2)}) collective-permute-start(f32[9,1152]{1,0:T(8,128)S(1)} %concatenate.129), channel_id=1, source_target_pairs={{0,1},{1,0},{2,3},{3,2},{4,5},{5,4},{6,7},{7,6},{8,9},{9,8},{10,11... | collective-permute-start | bytes 124424 | tf_op jit(solution)/shard_map/ppermute | solution.py:315
  378.4 2.3 collective-permute-start.10
  380.7 60.8 %collective-permute-start.14 = (bf16[1152,1152]{1,0:T(8,128)(2,1)}, bf16[1152,1152]{1,0:T(8,128)(2,1)}, u32[]{:S(2)}, u32[]{:S(2)}) collective-permute-start(bf16[1152,1152]{1,0:T(8,128)(2,1)} %convolution_convert_fusion.3), channel_id=1, source_target_pairs={{0,2},{1,3},{2,0},{3,1},{4,6},{5,7},{6,4},{7,5},{8,10},{9,11},{10,... | collective-permute-start | bytes 7962632 | tf_op jit(solution)/shard_map/ppermute | solution.py:315
  384.1 18.4 %collective-permute-start.20 = (bf16[528,1728]{1,0:T(8,128)(2,1)}, bf16[528,1728]{1,0:T(8,128)(2,1)S(1)}, u32[]{:S(2)}, u32[]{:S(2)}) collective-permute-start(bf16[528,1728]{1,0:T(8,128)(2,1)} %bitcast.49), channel_id=1, source_target_pairs={{0,1},{1,0},{2,3},{3,2},{4,5},{5,4},{6,7},{7,6},{8,9},{9,8},{10,11... | collective-permute-start | bytes 5474312 | tf_op jit(solution)/shard_map/ppermute | solution.py:315
  384.2 270.0 %collective-permute-start.11 = (bf16[2,528,288]{1,2,0:T(8,128)(2,1)}, bf16[2,528,288]{1,2,0:T(8,128)(2,1)}, u32[]{:S(2)}, u32[]{:S(2)}) collective-permute-start(bf16[2,528,288]{1,2,0:T(8,128)(2,1)} %copy.85), channel_id=1, source_target_pairs={{0,2},{1,3},{2,0},{3,1},{4,6},{5,7},{6,4},{7,5},{8,10},{9,11},{10,... | collective-permute-start | bytes 1824776 | tf_op jit(solution)/shard_map/ppermute | solution.py:315
  392.6 10.0 %copy-start.39 = (bf16[2,264,1728]{2,1,0:T(8,128)(2,1)S(1)}, bf16[2,264,1728]{2,1,0:T(8,128)(2,1)}, u32[]{:S(2)}) copy-start(bf16[2,264,1728]{2,1,0:T(8,128)(2,1)} %copy-done.38) | copy-start | bytes 5474308
  392.6 10.0 %copy-start.66 = (bf16[1056,1152]{1,0:T(8,128)(2,1)S(1)}, bf16[1056,1152]{1,0:T(8,128)(2,1)}, u32[]{:S(2)}) copy-start(bf16[1056,1152]{1,0:T(8,128)(2,1)} %pad_maximum_fusion.4) | copy-start | bytes 7299076
  392.6 31.2 %collective-permute-start.18 = (bf16[576,1152]{1,0:T(8,128)(2,1)S(1)}, bf16[576,1152]{1,0:T(8,128)(2,1)S(1)}, u32[]{:S(2)}, u32[]{:S(2)}) collective-permute-start(bf16[576,1152]{1,0:T(8,128)(2,1)S(1)} %dynamic-slice_bitcast_fusion), channel_id=1, source_target_pairs={{0,4},{4,0},{8,12},{12,8},{16,20},{20,16},{24,28},{28,24},{1,5},{5... | collective-permute-start | bytes 3981320 | tf_op jit(solution)/shard_map/ppermute | solution.py:315
  423.9 17.6 %copy-start.63 = (bf16[1152,1152]{1,0:T(8,128)(2,1)S(1)}, bf16[1152,1152]{1,0:T(8,128)(2,1)}, u32[]{:S(2)}) copy-start(bf16[1152,1152]{1,0:T(8,128)(2,1)} %convolution_convert_fusion.1) | copy-start | bytes 7962628
  424.3 21.2 %collective-permute-start.22 = (bf16[288,1152]{1,0:T(8,128)(2,1)S(1)}, bf16[288,1152]{1,0:T(8,128)(2,1)S(1)}, u32[]{:S(2)}, u32[]{:S(2)}) collective-permute-start(bf16[288,1152]{1,0:T(8,128)(2,1)S(1)} %dynamic-slice_bitcast_fusion.5), channel_id=1, source_target_pairs={{0,8},{4,12},{8,0},{12,4},{16,24},{20,28},{24,16},{28,20},{1,9},{5... | collective-permute-start | bytes 1990664 | tf_op jit(solution)/shard_map/ppermute | solution.py:315
  (75 other events, 250.1 us)

commit v2 on v1

--- a/solution.py
+++ b/solution.py
@@ -306,8 +306,6 @@
 GRAD_ROWS = 24
 CORE = ("tp", 1)
 ACROSS_Y = ("tp", 2)
-ACROSS_X = ("dp", 1)
-ACROSS_Z = ("dp", 2)
 
 
 def swap(value, link):
@@ -318,11 +316,6 @@
 def side(link):
     axis, bit = link
     return (lax.axis_index(axis) // bit) % 2
-
-
-def in_order(bit, mine, theirs):
-    flip = bit == 1
-    return jnp.stack([jnp.where(flip, theirs, mine), jnp.where(flip, mine, theirs)])
 
 
 def pick(value, index):
@@ -465,17 +458,16 @@
 
 
 def reduce_kernel(sizes, views, n_arrays, *refs):
-    ready, arrays, blocks, quarter = refs[0], refs[1 : 1 + n_arrays], refs[1 + n_arrays], refs[2 + n_arrays]
-    refs = refs[3 + n_arrays :]
+    ready, arrays, blocks = refs[0], refs[1 : 1 + n_arrays], refs[1 + n_arrays]
+    refs = refs[2 + n_arrays :]
     outs, refs = refs[: 1 + len(views)], refs[1 + len(views) :]
-    from_core, y_blocks, own_quarter, z_quarter, x_quarters = refs[:5]
-    total, from_y, from_one, half, from_two, from_far, final, part, far_part = refs[5:14]
-    y_sem, one_sem, two_sem, far_sem, back_two, back_one, block_sem, load_sem, out_sem = refs[14:]
+    from_core, y_blocks = refs[:2]
+    total, from_y, from_one, half, from_two, from_far, final = refs[2:9]
+    y_sem, one_sem, two_sem, far_sem, back_two, back_one, block_sem, load_sem, out_sem = refs[9:]
     chunks, n_ready = total.shape[0], sizes[0]
     dp, tp = lax.axis_index("dp"), lax.axis_index("tp")
     to_core, to_y, to_far = {"tp": peer(tp, 1)}, {"tp": peer(tp, 2)}, {"dp": peer(dp, 4)}
-    to_x, to_z = {"dp": peer(dp, 1)}, {"dp": peer(dp, 2)}
-    greet((to_core, to_y, to_x, to_z, to_far))
+    greet((to_core, to_y, {"dp": peer(dp, 1)}, {"dp": peer(dp, 2)}, to_far))
 
     def plan(s):
         z_first = (s % 4) // 3
@@ -518,22 +510,15 @@
 
             at += size
 
-    quarter_load = pltpu.make_async_copy(quarter, part, load_sem.at[0])
-    ready_load = pltpu.make_async_copy(ready, total.at[pl.ds(0, n_ready)], load_sem.at[1])
+    ready_load = pltpu.make_async_copy(ready, total.at[pl.ds(0, n_ready)], load_sem.at[0])
     ready_load.start()
-    quarter_load.start()
     core_blocks = [send(blocks.at[2 + k], from_core.at[k], block_sem, k, to_core) for k in range(2)]
     own_block = send(blocks.at[1], y_blocks.at[0], block_sem, 2, to_y)
     core_block = send(from_core.at[1], y_blocks.at[1], block_sem, 3, to_y)
-    quarter_far = send(quarter, far_part, block_sem, 4, to_far)
-    quarter_z = send(own_quarter, z_quarter, block_sem, 5, to_z)
-    quarter_x = send(own_quarter, x_quarters.at[0], block_sem, 6, to_x)
-    quarter_zx = send(z_quarter, x_quarters.at[1], block_sem, 7, to_x)
-    quarter_out = pltpu.make_async_copy(part, own_quarter, out_sem.at[chunks])
     loads, at = [], n_ready
     for k, (size, (a, mine, theirs)) in enumerate(zip(sizes[1:], views)):
         source = arrays[a].at[mine]
-        loads.append(pltpu.make_async_copy(source, total.at[pl.ds(at, size)], load_sem.at[2 + k]))
+        loads.append(pltpu.make_async_copy(source, total.at[pl.ds(at, size)], load_sem.at[1 + k]))
         loads[-1].start()
         for r in range(size):
             y_copy(at + r, arrays[a].at[theirs + (r,)]).start()
@@ -541,8 +526,7 @@
     for copy in core_blocks:
         copy.start()
     own_block.start()
-    quarter_far.start()
-    for copy in [ready_load, quarter_load] + loads:
+    for copy in [ready_load] + loads:
         copy.wait()
 
     def plus(left, right):
@@ -598,23 +582,6 @@
                 copy.wait_recv()
             core_block.start()
 
-        @pl.when(t == 8)
-        def _():
-            quarter_far.wait()
-            part[...] = plus(part[...], far_part[...])
-            quarter_out.start()
-
-        @pl.when(t == 9)
-        def _():
-            quarter_out.wait()
-            quarter_z.start()
-            quarter_x.start()
-
-        @pl.when(t == 18)
-        def _():
-            quarter_z.wait_recv()
-            quarter_zx.start()
-
         return carry
 
     lax.fori_loop(0, chunks + 7, step, 0)
@@ -636,12 +603,9 @@
         copy.wait_send()
     own_block.wait()
     core_block.wait()
-    quarter_z.wait_send()
-    quarter_x.wait()
-    quarter_zx.wait()
-
-
-def reduce_grads(ready, arrays, views, blocks, quarter):
+
+
+def reduce_grads(ready, arrays, views, blocks):
     sizes = (ready.shape[0],) + tuple(arrays[a].shape[len(mine)] for a, mine, _ in views)
     chunks = sum(sizes)
     rows, width = ready.shape[-2:]
@@ -650,12 +614,11 @@
     two_blocks = jax.ShapeDtypeStruct((2,) + blocks.shape[1:], blocks.dtype)
     hbm = pl.BlockSpec(memory_space=pltpu.MemorySpace.HBM)
     vmem = lambda *lead: pltpu.VMEM(lead + (rows, width), kind)
-    n_in, n_out = 3 + len(arrays), 6 + len(views)
+    n_in, n_out = 2 + len(arrays), 3 + len(views)
     return pl.pallas_call(
         functools.partial(reduce_kernel, sizes, views, len(arrays)),
         out_shape=[jax.ShapeDtypeStruct((n, 2, 2, rows, width), kind) for n in sizes]
-        + [two_blocks, two_blocks]
-        + [jax.ShapeDtypeStruct(lead + quarter.shape, kind) for lead in ((), (), (2,))],
+        + [two_blocks, two_blocks],
         in_specs=[hbm] * n_in,
         out_specs=[hbm] * n_out,
         scratch_shapes=[
@@ -666,23 +629,21 @@
             vmem(chunks),
             vmem(chunks),
             vmem(chunks, 2, 2),
-            pltpu.VMEM(quarter.shape, kind),
-            pltpu.VMEM(quarter.shape, kind),
             sem(chunks - sizes[0]),
             sem(chunks),
             sem(chunks),
             sem(chunks),
             sem(chunks),
             sem(chunks),
-            sem(8),
-            pltpu.SemaphoreType.DMA((2 + len(views),)),
-            pltpu.SemaphoreType.DMA((chunks + 1,)),
+            sem(4),
+            pltpu.SemaphoreType.DMA((1 + len(views),)),
+            pltpu.SemaphoreType.DMA((chunks,)),
         ],
         compiler_params=pltpu.CompilerParams(
             collective_id=2, has_side_effects=True, vmem_limit_bytes=56 * 2**20
         ),
         name="reduce_grads",
-    )(ready, *arrays, blocks, quarter)
+    )(ready, *arrays, blocks)
 
 
 def add_low(mine, theirs):
@@ -1017,7 +978,7 @@
     vectors = jnp.concatenate(
         [jnp.stack([b_skip, ln1_gain, ln1_bias, b_proj, ln2_gain, ln2_bias, b_down]), b_up.reshape(4, local)]
     )
-    y, core, x, z = side(ACROSS_Y), side(CORE), side(ACROSS_X), side(ACROSS_Z)
+    y, core = side(ACROSS_Y), side(CORE)
     cut = 2 * local
     tokens, cot_tokens = spread(main, long_skip, cotangent)
     tokens = tokens.reshape((2, 2) + tokens.shape[1:])
@@ -1104,10 +1065,6 @@
     def weight_grad(left, right):
         return low(dot("tf,tc->fc", left, right))
 
-    def split(value, bit):
-        halves = value.reshape(2, -1, width)
-        return pick(halves, bit), pick(halves, 1 - bit)
-
     result, d_n2 = stream_two + b_down_all, None
     acts, d_up, g_b_up = [None] * 4, [None] * 4, [None] * 4
     wd = [w_down, None, wd_core, None]
@@ -1125,7 +1082,7 @@
     down_theirs = weight_grad(both(acts[1], other(acts[3])), grad_both)
     down_come = swap(down_theirs, ACROSS_Y)
     up_theirs = weight_grad(n2_both, after(both(d_up[1], other(d_up[3])), down_theirs))
-    up_come = swap(up_theirs, ACROSS_Y)
+    up_come = swap(up_theirs[:cut], ACROSS_Y)
     d_n2, result, acts[0], d_up[0], up_theirs = meet(d_n2, result, acts[0], d_up[0], up_theirs)
     g_b_up = jnp.concatenate(g_b_up)
     down_mine = weight_grad(both(acts[0], other(acts[2])), grad_both)
@@ -1152,17 +1109,11 @@
     g_b_skip = jnp.sum(d_stream.astype(jnp.float32), 0)
     d_skip = low(dot("tc,fc->tf", d_stream, wskip))
     d_blocks = jnp.stack(jnp.split(d_skip, 4, 1))
-    down_come, d_blocks, proj_part, n1_both = meet(down_come, d_blocks, proj_part, n1_both)
-    down_keep, down_send = split(add_low(down_mine, down_come), x)
-    down_come = swap(down_send, ACROSS_X)
     qkv_part = chunked(weight_grad(both(d_own, other(d_partner)), n1_both), (3, 2))
     skip_part = chunked(weight_grad(skip_both, d_stream_both), (2,))
-    down_come, skip_part, qkv_part = meet(down_come, skip_part, qkv_part)
-    down_keep, down_send = split(add_low(down_keep, down_come), z)
-    down_come = swap(down_send, ACROSS_Z)
-    up_come, skip_part = meet(up_come, skip_part)
-    down_quarter = add_low(down_keep, down_come)
-    ready = chunked(add_low(up_mine, up_come), ())
+    up_part = chunked(jnp.stack([up_mine[cut:], up_theirs[cut:]]), (2,))
+    down_come, up_come, skip_part = meet(down_come, up_come, skip_part)
+    ready = chunked(jnp.concatenate([add_low(down_mine, down_come), add_low(up_mine[:cut], up_come)]), ())
 
     small = jnp.stack([g_b_skip, g_ln1_gain, g_ln1_bias, g_b_proj, g_ln2_gain, g_ln2_bias, g_b_down])
     arrived = other(jnp.concatenate([small, g_b_up[2:]]))
@@ -1174,19 +1125,22 @@
         return jnp.pad(flat, (0, 4 * GRAD_ROWS * width - flat.size)).reshape(1, 2, 2, GRAD_ROWS, width)
 
     vector_part = low(jnp.stack([vector_rows(rank, 0), vector_rows(peer(rank, 2), 1)]))
-    g_w_up, *sums = reduce_grads(
+    g_ready, *sums = reduce_grads(
         ready,
-        [proj_part, qkv_part, vector_part, skip_part],
-        [(0, (0,), (1,)), (1, (0, 0), (0, 1)), (1, (1, 0), (1, 1)), (1, (2, 0), (2, 1)), (2, (0,), (1,)), (3, (0,), (1,))],
+        [up_part, proj_part, qkv_part, vector_part, skip_part],
+        [(0, (0,), (1,)), (1, (0,), (1,))]
+        + [(2, (e, 0), (e, 1)) for e in range(3)]
+        + [(3, (0,), (1,)), (4, (0,), (1,))],
         d_blocks,
-        down_quarter,
-    )
-    *sums, from_core, y_blocks, down_quarter, z_quarter, x_quarters = sums
+    )
+    *sums, from_core, y_blocks = sums
     out_y, y_blocks = meet(out_y, y_blocks)
     (out,) = unspread(outs[0], out_core[0], out_y, 1)
     wide = lambda value: value.reshape(-1, width).astype(jnp.float32)
-    g_w_down = wide(in_order(x, in_order(z, down_quarter, z_quarter), in_order(z, x_quarters[0], x_quarters[1])))
-    g_w_proj, g_q, g_k, g_v, vectors, g_skip = (wide(g) for g in sums)
+    g_ready = g_ready.reshape(-1, width)
+    g_w_down = wide(g_ready[:width])
+    g_up_low, g_w_proj, g_q, g_k, g_v, vectors, g_skip = (wide(g) for g in sums)
+    g_w_up = jnp.concatenate([wide(g_ready[width:]), g_up_low])
     g_w_qkv = jnp.stack([g.T for g in (g_q, g_k, g_v)])
     vectors = vectors.reshape(-1)
     mine = vectors[: 7 * local].reshape(7, local)
@@ -1206,7 +1160,7 @@
         mine[3],
         mine[4],
         mine[5],
-        wide(g_w_up),
+        g_w_up,
         vectors[7 * local : 7 * local + width],
         g_w_down,
         mine[6],

time: 681 us -> 681 us (level)
  waiting for transfers between devices: 88.8 us -> 66.2 us
  local copies, waits for them, and re-layouts: 86.5 us -> 102 us
  Pallas kernels: 357 us -> 368 us
    ppermute x23 -> x21, waiting for transfers between devices: 88.8 us -> 66.2 us  [swap(): lax.ppermute(value, axis, [(i, i ^ bit) for i in range(lax.axis_size(axis...]
    pallas_call x1, Pallas kernels: 200 us -> 211 us  [reduce_grads(): pl.pallas_call(functools.partial(reduce_kernel, sizes, views, len(arrays)...]
    slice x0 -> x7, local copies, waits for them, and re-layouts: none -> 8.86 us  [the longest x1 3.49 us: body_rows(): g_w_down = wide(g_ready[:width])]
    unnamed x176 -> x188, local copies, waits for them, and re-layouts: 52.1 us -> 57.6 us
  transfers between devices with their start and end apart: 23 -> 21, of which waited for: 3 -> 2; matrix products, arithmetic and copies ran while one was open for 21% -> 21% of each run, Pallas kernels for 41% -> 43%
where the time goes in v2:
time: 681 us; the launch traced here: 676 us
  Pallas kernels  368 us (54%)
  local copies, waits for them, and re-layouts  102 us (15%)
  matrix products  85.9 us (13%)
  waiting for transfers between devices  66.2 us (10%)
  other arithmetic  42.7 us (6%)
  starting transfers between devices  9.48 us (1%)
    pallas_call x1, Pallas kernels, reduce_grads(): pl.pallas_call(functools.partial(reduce_kernel, sizes, views, len(arrays)...  211 us
    dot_general x17, matrix products, dot(): return jnp.einsum(spec, left, right, preferred_element_type=jnp.float32)  85.9 us
    pallas_call x1, Pallas kernels, gather_weights(): pl.pallas_call(functools.partial(gather_kernel, pieces, len(arrays), len(...  74.2 us
    ppermute x21, waiting for transfers between devices, swap(): lax.ppermute(value, axis, [(i, i ^ bit) for i in range(lax.axis_size(axis...  66.2 us
    unnamed x188, local copies, waits for them, and re-layouts  57.6 us
    pallas_call x4, Pallas kernels, feed(): pl.pallas_call(functools.partial(feed_kernel, d_n is None), grid=(hidden...  47.5 us
    pallas_call x1, Pallas kernels, attention_back(): pl.pallas_call(attend_back_kernel, out_shape=[shape(cols)] * 3 + [shape(3...  20.5 us
  transfers between devices with their start and end apart: 21, of which 2 were waited for; matrix products, arithmetic and copies ran while one was open for 21% of the time, Pallas kernels for 43%

profile of v2, /device:TPU:0, one launch (start us, length us, event | category | flops | bytes accessed | tf_op | source)
XLA Modules:
  0.0 676.1 jit_solution(6898558398157408336)
XLA Ops:
  24.0 74.2 %gather_weights.1 = (bf16[2,528,576]{2,1,0:T(8,128)(2,1)S(1)}, bf16[528,576]{1,0:T(8,128)(2,1)S(1)}, bf16[528,576]{1,0:T(8,128)(2,1)S(1)}, f32[11,288]{1,0:T(8,1...) custom-call(bf16[2,2,528,576]{3,2,1,0:T(8,128)(2,1)} %bitcast.127, ...), custom_call_target="tpu_custom_call" | custom-call | tf_op jit(solution)/shard_map/gather_weights/pallas_call | solution.py:447
  112.6 5.8 concatenate.94
  122.5 8.1 %convolution_add_fusion.3 = f32[528,1152]{1,0:T(8,128)} fusion(bf16[528,2304]{1,0:T(8,128)(2,1)} %concatenate.94, bf16[2304,1152]{1,0:T(8,128)(2,1)} %bitcast.175, f32[1152]{0:T(1024)S(1)} %get-tuple-element.261), kind=kOutput, calls=%fused_computation.15 | convolution fusion | flops 2803451904 | bytes 10179072 | tf_op jit(solution)/shard_map/td,dc->tc/dot_general | solution.py:770
  133.0 3.4 fusion.6
  136.4 58.1 %collective-permute-done = bf16[2,528,288]{1,2,0:T(8,128)(2,1)} collective-permute-done((bf16[2,528,288]{1,2,0:T(8,128)(2,1)}, bf16[2,528,288]{1,2,0:T(8,128)(2,1)}, u32[]{:S(2)}, u32[]{:S(2)}) %collective-permute-start) | collective-permute-done | bytes 608288 | tf_op jit(solution)/shard_map/ppermute | solution.py:313
  199.4 3.4 convolution_convert_fusion.9
  202.8 3.7 convolution_convert_fusion.10
  206.5 3.7 convolution_convert_fusion.11
  210.3 9.6 %attend.1 = (bf16[2,264,1152]{2,1,0:T(8,128)(2,1)S(1)}, f32[2,16,264]{2,1,0:T(8,128)S(1)}) custom-call(bf16[2,264,1152]{2,1,0:T(8,128)(2,1)S(1)} %bitcast.154, bf16[2,264,1152]{2,1,0:T(8,128)(2,1)S(1)} %bitcast.152, bf16[2,264,1152]{2,1,0:T(8,128)(2,1)S(1)} %bitcast.150), custom_call_target="tpu_custom_call" | custom-call | flops 642318336 | bytes 4866048 | tf_op jit(solution)/shard_map/attend/pallas_call | solution.py:860
  219.9 3.4 fusion.3
  227.0 3.4 pad_maximum_fusion.5
  231.4 12.1 %feed.4 = (bf16[528,1152]{1,0:T(8,128)(2,1)S(1)}, bf16[528,1152]{1,0:T(8,128)(2,1)S(1)}, f32[1,1152]{1,0:T(1,128)S(1)}, f32[528,1152]{1,0:T(8,128)S(1)}, f32[528,1152]{1,0:T(8,128)S(1)}) custom-call(bf16[528,1152]{1,0:T(8,128)(2,1)S(1)} %get-tuple-element.276.n_ref, bf16[528,1152]{1,0:T(8,128)(2,1)} %arrange.1.g_ref, bf16[1152,1152]{1,0:T(8,128)(2,1)} %bitcast.148, ...), custom_call_target="tpu_custom_call" | custom-call | flops 7007109120 | bytes 5308416 | tf_op jit(solution)/shard_map/feed/pallas_call | solution.py:924
  244.6 12.0 %feed.5 = (bf16[528,1152]{1,0:T(8,128)(2,1)}, bf16[528,1152]{1,0:T(8,128)(2,1)}, f32[1,1152]{1,0:T(1,128)S(1)}, f32[528,1152]{1,0:T(8,128)S(1)}, f32[528,1152]{1,0:T(8,128)S(1)}) custom-call(bf16[528,1152]{1,0:T(8,128)(2,1)S(1)} %get-tuple-element.276.n_ref, bf16[528,1152]{1,0:T(8,128)(2,1)} %arrange.1.g_ref, bf16[1152,1152]{1,0:T(8,128)(2,1)} %bitcast.178, ...), custom_call_target="tpu_custom_call" | custom-call | flops 7007109120 | bytes 5308416 | tf_op jit(solution)/shard_map/feed/pallas_call | solution.py:924
  263.6 11.7 %feed.6 = (bf16[528,1152]{1,0:T(8,128)(2,1)S(1)}, bf16[528,1152]{1,0:T(8,128)(2,1)S(1)}, f32[1,1152]{1,0:T(1,128)S(1)}, f32[528,1152]{1,0:T(8,128)S(1)}, f32[528,1152]{1,0:T(8,128)S(1)}) custom-call(bf16[528,1152]{1,0:T(8,128)(2,1)S(1)} %get-tuple-element.276.n_ref, bf16[528,1152]{1,0:T(8,128)(2,1)} %arrange.1.g_ref, bf16[1152,1152]{1,0:T(8,128)(2,1)} %bitcast.147, ...), custom_call_target="tpu_custom_call" | custom-call | flops 7007109120 | bytes 5308416 | tf_op jit(solution)/shard_map/feed/pallas_call | solution.py:924
  278.7 11.7 %feed.7 = (bf16[528,1152]{1,0:T(8,128)(2,1)}, bf16[528,1152]{1,0:T(8,128)(2,1)}, f32[1,1152]{1,0:T(1,128)S(1)}, f32[528,1152]{1,0:T(8,128)S(1)}, f32[528,1152]{1,0:T(8,128)S(1)}) custom-call(bf16[528,1152]{1,0:T(8,128)(2,1)S(1)} %copy-done.17, bf16[528,1152]{1,0:T(8,128)(2,1)} %arrange.1.g_ref, bf16[1152,1152]{1,0:T(8,128)(2,1)} %bitcast.177, ...), custom_call_target="tpu_custom_call" | custom-call | flops 7007109120 | bytes 5308416 | tf_op jit(solution)/shard_map/feed/pallas_call | solution.py:924
  293.2 2.8 fusion.49
  296.5 7.7 %convolution_convert_fusion.4 = bf16[1152,1152]{1,0:T(8,128)(2,1)} fusion(bf16[528,1152]{1,0:T(8,128)(2,1)} %collective-permute-done.8, bf16[528,1152]{1,0:T(8,128)(2,1)S(1)} %copy-done.52, bf16[528,1152]{1,0:T(8,128)(2,1)} %collective-permute-done.9, bf16[528,1152]{1,0:T(8,128)(2,1)} %arrange.1.g_ref), kind=kOutput, calls=%fused_computation.4 | convolution fusion | flops 2813902848 | bytes 7520256 | tf_op jit(solution)/shard_map/tf,tc->fc/dot_general | solution.py:770
  305.8 4.0 convolution_convert_fusion.3
  313.7 3.5 convert_reduce_fusion
  317.3 3.3 convolution_convert_fusion.8
  322.7 20.5 %attend_back.1 = (bf16[2,264,1152]{2,1,0:T(8,128)(2,1)S(1)}, bf16[2,264,1152]{2,1,0:T(8,128)(2,1)S(1)}, bf16[2,264,1152]{2,1,0:T(8,128)(2,1)S(1)}, bf16[2,264,17...) custom-call(bf16[2,264,1152]{2,1,0:T(8,128)(2,1)S(1)} %bitcast.155, bf16[2,264,1152]{2,1,0:T(8,128)(2,1)S(1)} %bitcast.153, ...), custom_call_target="tpu_custom_call" | custom-call | flops 1605795840 | bytes 8515584 | tf_op jit(solution)/shard_map/attend_back/pallas_call | solution.py:879
  350.6 3.3 convert_reduce_fusion.2
  356.1 6.2 convolution_convert_fusion.6
  364.3 5.5 convolution_convert_fusion.1
  369.8 8.4 %convolution_convert_fusion.2 = bf16[1152,1152]{1,0:T(8,128)(2,1)} fusion(bf16[528,1152]{1,0:T(8,128)(2,1)} %collective-permute-done.12, bf16[528,1152]{1,0:T(8,128)(2,1)S(1)} %copy-done.54, bf16[528,1152]{1,0:T(8,128)(2,1)} %collective-permute-done.9, bf16[528,1152]{1,0:T(8,128)(2,1)} %arrange.1.g_ref), kind=kOutput, calls=%fused_computation.2 | convolution fusion | flops 2813902848 | bytes 7520256 | tf_op jit(solution)/shard_map/tf,tc->fc/dot_general | solution.py:770
  395.5 7.8 %convolution_convert_fusion = bf16[1152,1152]{1,0:T(8,128)(2,1)} fusion(bf16[1056,1152]{1,0:T(8,128)(2,1)} %fusion.6, bf16[528,1152]{1,0:T(8,128)(2,1)} %collective-permute-done.16, bf16[528,1152]{1,0:T(8,128)(2,1)} %get-tuple-element.267), kind=kOutput, calls=%fused_computation | convolution fusion | flops 2809036800 | bytes 7520256 | tf_op jit(solution)/shard_map/tf,tc->fc/dot_general | solution.py:770
  404.0 5.1 convolution_convert_fusion.7
  409.2 9.1 %convolution_convert_fusion.5 = bf16[1728,1152]{1,0:T(8,128)(2,1)} fusion(bf16[1056,1152]{1,0:T(8,128)(2,1)S(1)} %copy-done.70, bf16[528,1728]{1,0:T(8,128)(2,1)} %collective-permute-done.19, bf16[528,1728]{1,0:T(8,128)(2,1)S(1)} %bitcast.149), kind=kOutput, calls=%fused_computation.5 | convolution fusion | flops 4213555200 | bytes 10063872 | tf_op jit(solution)/shard_map/tf,tc->fc/dot_general | solution.py:770
  418.4 8.0 %collective-permute-done.15 = bf16[576,1152]{1,0:T(8,128)(2,1)S(1)} collective-permute-done((bf16[576,1152]{1,0:T(8,128)(2,1)}, bf16[576,1152]{1,0:T(8,128)(2,1)S(1)}, u32[]{:S(2)}, u32[]{:S(2)}) %collective-permute-start.15) | collective-permute-done | bytes 1327136 | tf_op jit(solution)/shard_map/ppermute | solution.py:313
  431.4 210.9 %reduce_grads.1 = (bf16[18,2,2,24,1152]{4,3,2,1,0:T(8,128)(2,1)}, bf16[6,2,2,24,1152]{4,3,2,1,0:T(8,128)(2,1)}, bf16[3,2,2,24,1152]{4,3,2,1,0:T(8,128)(2,1)}, bf...) custom-call(bf16[18,2,2,24,1152]{4,3,2,1,0:T(8,128)(2,1)} %bitcast.1, ...), custom_call_target="tpu_custom_call" | custom-call | tf_op jit(solution)/shard_map/reduce_grads/pallas_call | solution.py:618
  644.8 3.5 slice.202
  660.1 4.6 bitcast_convert_fusion
  (335 shorter events, 134.7 us)
Async XLA Ops:
  118.4 126.2 %collective-permute-start.4 = (bf16[1152,1152]{1,0:T(8,128)(2,1)}, bf16[1152,1152]{1,0:T(8,128)(2,1)}, u32[]{:S(2)}, u32[]{:S(2)}) collective-permute-start(bf16[1152,1152]{1,0:T(8,128)(2,1)} %down_ref.1), channel_id=1, source_target_pairs={{0,1},{1,0},{2,3},{3,2},{4,5},{5,4},{6,7},{7,6},{8,9},{9,8},{10,11... | collective-permute-start | bytes 7962632 | tf_op jit(solution)/shard_map/ppermute | solution.py:313
  118.8 140.7 %collective-permute-start.3 = (bf16[1152,1152]{1,0:T(8,128)(2,1)}, bf16[1152,1152]{1,0:T(8,128)(2,1)}, u32[]{:S(2)}, u32[]{:S(2)}) collective-permute-start(bf16[1152,1152]{1,0:T(8,128)(2,1)} %down_ref.1), channel_id=1, source_target_pairs={{0,2},{1,3},{2,0},{3,1},{4,6},{5,7},{6,4},{7,5},{8,10},{9,11},{10,... | collective-permute-start | bytes 7962632 | tf_op jit(solution)/shard_map/ppermute | solution.py:313
  120.6 74.0 %collective-permute-start = (bf16[2,528,288]{1,2,0:T(8,128)(2,1)}, bf16[2,528,288]{1,2,0:T(8,128)(2,1)}, u32[]{:S(2)}, u32[]{:S(2)}) collective-permute-start(bf16[2,528,288]{1,2,0:T(8,128)(2,1)} %bitcast.1), channel_id=1, source_target_pairs={{0,2},{1,3},{2,0},{3,1},{4,6},{5,7},{6,4},{7,5},{8,10},{9,11},{10,... | collective-permute-start | bytes 1824776 | tf_op jit(solution)/shard_map/ppermute | solution.py:313
  122.5 10.5 %copy-start.61 = (bf16[528,576]{1,0:T(8,128)(2,1)S(1)}, bf16[528,576]{1,0:T(8,128)(2,1)}, u32[]{:S(2)}) copy-start(bf16[528,576]{1,0:T(8,128)(2,1)} %get-tuple-element.282) | copy-start | bytes 1824772
  122.5 10.5 %copy-start.62 = (bf16[528,576]{1,0:T(8,128)(2,1)S(1)}, bf16[528,576]{1,0:T(8,128)(2,1)}, u32[]{:S(2)}) copy-start(bf16[528,576]{1,0:T(8,128)(2,1)} %get-tuple-element.269) | copy-start | bytes 1824772
  122.5 10.5 %copy-start.68 = (bf16[528,576]{1,0:T(8,128)(2,1)S(1)}, bf16[528,576]{1,0:T(8,128)(2,1)}, u32[]{:S(2)}) copy-start(bf16[528,576]{1,0:T(8,128)(2,1)} %get-tuple-element.281) | copy-start | bytes 1824772
  133.0 62.8 %copy-start.72 = (bf16[1,1,528,288]{2,3,1,0:T(8,128)(2,1)S(1)}, bf16[1,1,528,288]{2,3,1,0:T(8,128)(2,1)}, u32[]{:S(2)}) copy-start(bf16[1,1,528,288]{2,3,1,0:T(8,128)(2,1)} %copy.78) | copy-start | bytes 912388
  136.4 60.3 %copy-start.59 = (f32[528,1152]{1,0:T(8,128)S(1)}, f32[528,1152]{1,0:T(8,128)}, u32[]{:S(2)}) copy-start(f32[528,1152]{1,0:T(8,128)} %convolution_add_fusion.3) | copy-start | bytes 7299076
  196.7 26.8 %collective-permute-start.2 = (bf16[2,528,288]{1,2,0:T(8,128)(2,1)}, bf16[2,528,288]{1,2,0:T(8,128)(2,1)}, u32[]{:S(2)}, u32[]{:S(2)}) collective-permute-start(bf16[2,528,288]{1,2,0:T(8,128)(2,1)} %pad_maximum_fusion.14), channel_id=1, source_target_pairs={{0,1},{1,0},{2,3},{3,2},{4,5},{5,4},{6,7},{7,6},{8,9},{9,8},{10,11... | collective-permute-start | bytes 1824776 | tf_op jit(solution)/shard_map/ppermute | solution.py:313
  198.7 28.3 %collective-permute-start.1 = (bf16[528,1152]{1,0:T(8,128)(2,1)}, bf16[528,1152]{1,0:T(8,128)(2,1)}, u32[]{:S(2)}, u32[]{:S(2)}) collective-permute-start(bf16[528,1152]{1,0:T(8,128)(2,1)} %add_convert_fusion.3), channel_id=1, source_target_pairs={{0,1},{1,0},{2,3},{3,2},{4,5},{5,4},{6,7},{7,6},{8,9},{9,8},{10,11... | collective-permute-start | bytes 3649544 | tf_op jit(solution)/shard_map/ppermute | solution.py:313
  210.2 13.1 %copy-start.45 = (bf16[528,1152]{1,0:T(8,128)(2,1)}, bf16[528,1152]{1,0:T(8,128)(2,1)S(1)}, u32[]{:S(2)}) copy-start(bf16[528,1152]{1,0:T(8,128)(2,1)S(1)} %convolution_convert_fusion.11) | copy-start | bytes 3649540
  231.4 28.9 %copy-start.16 = (bf16[528,1152]{1,0:T(8,128)(2,1)}, bf16[528,1152]{1,0:T(8,128)(2,1)S(1)}, u32[]{:S(2)}) copy-start(bf16[528,1152]{1,0:T(8,128)(2,1)S(1)} %get-tuple-element.276.n_ref) | copy-start | bytes 3649540
  244.6 12.0 %copy-start.53 = (bf16[528,1152]{1,0:T(8,128)(2,1)}, bf16[528,1152]{1,0:T(8,128)(2,1)S(1)}, u32[]{:S(2)}) copy-start(bf16[528,1152]{1,0:T(8,128)(2,1)S(1)} %get-tuple-element.138) | copy-start | bytes 3649540
  259.5 17.9 %collective-permute-start.5 = (bf16[1152,1152]{1,0:T(8,128)(2,1)}, bf16[1152,1152]{1,0:T(8,128)(2,1)}, u32[]{:S(2)}, u32[]{:S(2)}) collective-permute-start(bf16[1152,1152]{1,0:T(8,128)(2,1)} %collective-permute-done.3.down_ref), channel_id=1, source_target_pairs={{0,1},{1,0},{2,3},{3,2},{4,5},{5,4},{6,7},{7,6},{8,9},{9,8},{10,11... | collective-permute-start | bytes 7962632 | tf_op jit(solution)/shard_map/ppermute | solution.py:313
  260.2 35.9 %collective-permute-start.9 = (bf16[528,1152]{1,0:T(8,128)(2,1)}, bf16[528,1152]{1,0:T(8,128)(2,1)}, u32[]{:S(2)}, u32[]{:S(2)}) collective-permute-start(bf16[528,1152]{1,0:T(8,128)(2,1)} %arrange.1.g_ref), channel_id=1, source_target_pairs={{0,1},{1,0},{2,3},{3,2},{4,5},{5,4},{6,7},{7,6},{8,9},{9,8},{10,11... | collective-permute-start | bytes 3649544 | tf_op jit(solution)/shard_map/ppermute | solution.py:313
  291.8 4.6 collective-permute-start.8
  292.3 11.8 %collective-permute-start.7 = (bf16[528,1152]{1,0:T(8,128)(2,1)}, bf16[528,1152]{1,0:T(8,128)(2,1)}, u32[]{:S(2)}, u32[]{:S(2)}) collective-permute-start(bf16[528,1152]{1,0:T(8,128)(2,1)} %get-tuple-element.131), channel_id=1, source_target_pairs={{0,1},{1,0},{2,3},{3,2},{4,5},{5,4},{6,7},{7,6},{8,9},{9,8},{10,11... | collective-permute-start | bytes 3649544 | tf_op jit(solution)/shard_map/ppermute | solution.py:313
  292.6 13.1 %collective-permute-start.6 = (bf16[528,1152]{1,0:T(8,128)(2,1)}, bf16[528,1152]{1,0:T(8,128)(2,1)S(1)}, u32[]{:S(2)}, u32[]{:S(2)}) collective-permute-start(bf16[528,1152]{1,0:T(8,128)(2,1)} %copy-done.16), channel_id=1, source_target_pairs={{0,1},{1,0},{2,3},{3,2},{4,5},{5,4},{6,7},{7,6},{8,9},{9,8},{10,11... | collective-permute-start | bytes 3649544 | tf_op jit(solution)/shard_map/ppermute | solution.py:313
  295.9 67.1 %collective-permute-start.13 = (bf16[528,1152]{1,0:T(8,128)(2,1)}, bf16[528,1152]{1,0:T(8,128)(2,1)}, u32[]{:S(2)}, u32[]{:S(2)}) collective-permute-start(bf16[528,1152]{1,0:T(8,128)(2,1)} %get-tuple-element.141), channel_id=1, source_target_pairs={{0,1},{1,0},{2,3},{3,2},{4,5},{5,4},{6,7},{7,6},{8,9},{9,8},{10,11... | collective-permute-start | bytes 3649544 | tf_op jit(solution)/shard_map/ppermute | solution.py:313
  296.0 73.8 %collective-permute-start.12 = (bf16[528,1152]{1,0:T(8,128)(2,1)}, bf16[528,1152]{1,0:T(8,128)(2,1)}, u32[]{:S(2)}, u32[]{:S(2)}) collective-permute-start(bf16[528,1152]{1,0:T(8,128)(2,1)} %get-tuple-element.139), channel_id=1, source_target_pairs={{0,1},{1,0},{2,3},{3,2},{4,5},{5,4},{6,7},{7,6},{8,9},{9,8},{10,11... | collective-permute-start | bytes 3649544 | tf_op jit(solution)/shard_map/ppermute | solution.py:313
  309.8 11.0 %copy-start.66 = (bf16[1152,1152]{1,0:T(8,128)(2,1)}, bf16[1152,1152]{1,0:T(8,128)(2,1)S(1)}, u32[]{:S(2)}) copy-start(bf16[1152,1152]{1,0:T(8,128)(2,1)S(1)} %convolution_convert_fusion.3) | copy-start | bytes 7962628
  320.6 83.4 %collective-permute-start.18 = (bf16[528,1152]{1,0:T(8,128)(2,1)}, bf16[528,1152]{1,0:T(8,128)(2,1)}, u32[]{:S(2)}, u32[]{:S(2)}) collective-permute-start(bf16[528,1152]{1,0:T(8,128)(2,1)} %get-tuple-element.265), channel_id=1, source_target_pairs={{0,1},{1,0},{2,3},{3,2},{4,5},{5,4},{6,7},{7,6},{8,9},{9,8},{10,11... | collective-permute-start | bytes 3649544 | tf_op jit(solution)/shard_map/ppermute | solution.py:313
  322.0 104.4 %collective-permute-start.14 = (bf16[1152,1152]{1,0:T(8,128)(2,1)}, bf16[1152,1152]{1,0:T(8,128)(2,1)}, u32[]{:S(2)}, u32[]{:S(2)}) collective-permute-start(bf16[1152,1152]{1,0:T(8,128)(2,1)} %convolution_convert_fusion.4), channel_id=1, source_target_pairs={{0,2},{1,3},{2,0},{3,1},{4,6},{5,7},{6,4},{7,5},{8,10},{9,11},{10,... | collective-permute-start | bytes 7962632 | tf_op jit(solution)/shard_map/ppermute | solution.py:313
  322.7 20.5 %copy-start.33 = (bf16[4,2,2,72,1152]{4,3,2,1,0:T(8,128)(2,1)S(1)}, bf16[4,2,2,72,1152]{4,3,2,1,0:T(8,128)(2,1)}, u32[]{:S(2)}) copy-start(bf16[4,2,2,72,1152]{4,3,2,1,0:T(8,128)(2,1)} %copy-done.31) | copy-start | bytes 7962628
  354.0 40.1 %collective-permute-start.16 = (bf16[528,1152]{1,0:T(8,128)(2,1)}, bf16[528,1152]{1,0:T(8,128)(2,1)}, u32[]{:S(2)}, u32[]{:S(2)}) collective-permute-start(bf16[528,1152]{1,0:T(8,128)(2,1)} %get-tuple-element.267), channel_id=1, source_target_pairs={{0,1},{1,0},{2,3},{3,2},{4,5},{5,4},{6,7},{7,6},{8,9},{9,8},{10,11... | collective-permute-start | bytes 3649544 | tf_op jit(solution)/shard_map/ppermute | solution.py:313
  363.1 23.1 %collective-permute-start.20 = (f32[9,1152]{1,0:T(8,128)}, f32[9,1152]{1,0:T(8,128)}, u32[]{:S(2)}, u32[]{:S(2)}) collective-permute-start(f32[9,1152]{1,0:T(8,128)} %concatenate.112), channel_id=1, source_target_pairs={{0,1},{1,0},{2,3},{3,2},{4,5},{5,4},{6,7},{7,6},{8,9},{9,8},{10,11... | collective-permute-start | bytes 124424 | tf_op jit(solution)/shard_map/ppermute | solution.py:313
  384.5 24.7 %collective-permute-start.19 = (bf16[528,1728]{1,0:T(8,128)(2,1)}, bf16[528,1728]{1,0:T(8,128)(2,1)}, u32[]{:S(2)}, u32[]{:S(2)}) collective-permute-start(bf16[528,1728]{1,0:T(8,128)(2,1)} %bitcast.46), channel_id=1, source_target_pairs={{0,1},{1,0},{2,3},{3,2},{4,5},{5,4},{6,7},{7,6},{8,9},{9,8},{10,11... | collective-permute-start | bytes 5474312 | tf_op jit(solution)/shard_map/ppermute | solution.py:313
  386.2 4.1 collective-permute-start.10
  391.2 12.1 %collective-permute-start.17 = (bf16[528,576]{1,0:T(8,128)(2,1)}, bf16[528,576]{1,0:T(8,128)(2,1)}, u32[]{:S(2)}, u32[]{:S(2)}) collective-permute-start(bf16[528,576]{1,0:T(8,128)(2,1)} %get-tuple-element.287), channel_id=1, source_target_pairs={{0,1},{1,0},{2,3},{3,2},{4,5},{5,4},{6,7},{7,6},{8,9},{9,8},{10,11... | collective-permute-start | bytes 1824776 | tf_op jit(solution)/shard_map/ppermute | solution.py:313
  394.2 32.2 %collective-permute-start.15 = (bf16[576,1152]{1,0:T(8,128)(2,1)}, bf16[576,1152]{1,0:T(8,128)(2,1)S(1)}, u32[]{:S(2)}, u32[]{:S(2)}) collective-permute-start(bf16[576,1152]{1,0:T(8,128)(2,1)} %slice.216), channel_id=1, source_target_pairs={{0,2},{1,3},{2,0},{3,1},{4,6},{5,7},{6,4},{7,5},{8,10},{9,11},{10,... | collective-permute-start | bytes 3981320 | tf_op jit(solution)/shard_map/ppermute | solution.py:313
  403.3 247.8 %collective-permute-start.11 = (bf16[2,528,288]{1,2,0:T(8,128)(2,1)S(1)}, bf16[2,528,288]{1,2,0:T(8,128)(2,1)S(1)}, u32[]{:S(2)}, u32[]{:S(2)}) collective-permute-start(bf16[2,528,288]{1,2,0:T(8,128)(2,1)S(1)} %copy.85), channel_id=1, source_target_pairs={{0,2},{1,3},{2,0},{3,1},{4,6},{5,7},{6,4},{7,5},{8,10},{9,11},{10,... | collective-permute-start | bytes 1824776 | tf_op jit(solution)/shard_map/ppermute | solution.py:313
  409.2 17.2 %copy-start.65 = (bf16[1152,1152]{1,0:T(8,128)(2,1)S(1)}, bf16[1152,1152]{1,0:T(8,128)(2,1)}, u32[]{:S(2)}) copy-start(bf16[1152,1152]{1,0:T(8,128)(2,1)} %copy-done.64) | copy-start | bytes 7962628
  (81 other events, 255.0 us)
